TPU v7x, 1024 devices: a whole 4x8x16 slice. The times are simulated.
1024 devices in a mesh: lat: 16 (over x, z_hi), lon: 64 (over y, z_lo, core).
Axes of the slice: x: 4, y: 8, z: 16 (z_hi: 4, z_lo: 4; z = z_hi * 4 + z_lo), core: 2. Of those that a mesh axis runs over, the one named last changes fastest.
Arguments:
- queries: bfloat16 [8, 128, 256, 640], P(None, 'lat', 'lon'), may hold values from -12 to 12
- key_vectors: bfloat16 [8, 128, 256, 640], P(None, 'lat', 'lon'), may hold values from -12 to 12
- values: bfloat16 [8, 128, 256, 640], P(None, 'lat', 'lon'), may hold values from -6 to 6
- upstream: bfloat16 [8, 128, 256, 640], P(None, 'lat', 'lon'), may hold values from -6 to 6
Outputs:
- attended: bfloat16 [8, 128, 256, 640], P(None, 'lat', 'lon')
- grad_queries: bfloat16 [8, 128, 256, 640], P(None, 'lat', 'lon')
- grad_keys: bfloat16 [8, 128, 256, 640], P(None, 'lat', 'lon')
- grad_values: bfloat16 [8, 128, 256, 640], P(None, 'lat', 'lon')
All inputs are finite; a program needn't handle non-finite values.
Results may differ from a plain program's by a relative error of at most 0.0044.
The roundings to bfloat16 on the way count: a program that leaves them out, or rounds other values in their place, can miss the bound.
Values may be sent and summed in bfloat16 or wider, within the bound.
No kernel may reach another device: no remote copies, remote signals or barrier semaphores. Data moves between devices by JAX's collectives and lax.ppermute only.
A program may use at most 32 MiB of HBM per device.

v0:
```python
import jax
import jax.numpy as jnp
from jax import lax
from jax.sharding import PartitionSpec as P

HEAD_DIM = 64


def side_by_side(arrays, axis, split_dim, concat_dim, along):
    both = jnp.concatenate(arrays, axis=along)
    whole, at, finished = (
        lax.all_to_all(both, axis, split_axis=split_dim, concat_axis=concat_dim, tiled=True),
        0,
        [],
    )
    for a in arrays:
        finished.append(lax.slice_in_dim(whole, at, at + a.shape[along], axis=along))
        at += a.shape[along]
    return tuple(finished)


def split_heads(tensor):
    leading = tensor.shape[0] * tensor.shape[1]
    return tensor.reshape(leading, tensor.shape[2], tensor.shape[3] // HEAD_DIM, HEAD_DIM)


def merge_heads(tensor, like):
    return tensor.astype(jnp.bfloat16).reshape(like.shape)


def softmax_weights(query_heads, key_heads):
    scores = jnp.einsum(
        "nqhd,nkhd->nhqk", query_heads, key_heads, preferred_element_type=jnp.float32
    ) * HEAD_DIM ** (-0.5)
    return jax.nn.softmax(scores, axis=-1)


def gradient_terms(query_heads, key_heads, value_heads, grad_heads):
    score_scale = HEAD_DIM ** (-0.5)
    probs = softmax_weights(query_heads, key_heads)
    rounded = probs.astype(jnp.bfloat16)
    grad_probs = jnp.einsum(
        "nqhd,nkhd->nhqk", grad_heads, value_heads, preferred_element_type=jnp.float32
    )
    row_delta = jnp.sum(probs * grad_probs, axis=-1, keepdims=True)
    grad_scores = (probs * (grad_probs - row_delta)).astype(jnp.bfloat16)
    grad_value_heads = jnp.einsum(
        "nhqk,nqhd->nkhd", rounded, grad_heads, preferred_element_type=jnp.float32
    )
    grad_query_heads = (
        jnp.einsum("nhqk,nkhd->nqhd", grad_scores, key_heads, preferred_element_type=jnp.float32)
        * score_scale
    )
    grad_key_heads = (
        jnp.einsum("nhqk,nqhd->nkhd", grad_scores, query_heads, preferred_element_type=jnp.float32)
        * score_scale
    )
    return (rounded, grad_query_heads, grad_key_heads, grad_value_heads)


def joint_local(inputs):
    queries, key_vectors, values, upstream = inputs
    value_heads = split_heads(values)
    rounded, grad_q, grad_k, grad_v = gradient_terms(
        split_heads(queries), split_heads(key_vectors), value_heads, split_heads(upstream)
    )
    output = jnp.einsum("nhqk,nkhd->nqhd", rounded, value_heads, preferred_element_type=jnp.float32)
    return (
        merge_heads(output, queries),
        merge_heads(grad_q, queries),
        merge_heads(grad_k, queries),
        merge_heads(grad_v, queries),
    )


def lon_layout(tensor, groups):
    batch, rows, cols, feats = tensor.shape
    return tensor.reshape(groups, batch * rows // groups, cols, feats)


def lat_layout(tensor, groups):
    batch, rows, cols, feats = tensor.shape
    return tensor.transpose(0, 2, 1, 3).reshape(groups, batch * cols // groups, rows, feats)


def lon_restore(tensor, full_shape):
    return tensor.reshape(full_shape)


def lat_restore(tensor, full_shape):
    batch, rows, cols, feats = full_shape
    return tensor.reshape(batch, cols, rows, feats).transpose(0, 2, 1, 3)


def on_device(queries, key_vectors, values, upstream):
    full_shape = queries.shape
    lon_groups = lax.axis_size("lon")
    lat_groups = lax.axis_size("lat")
    inputs = (queries, key_vectors, values, upstream)
    lon_items = tuple((lon_layout(item, lon_groups) for item in inputs))
    lat_items = tuple((lat_layout(item, lat_groups) for item in inputs))
    lon_done = joint_local(
        (
            lax.all_to_all(lon_items[0], "lon", split_axis=0, concat_axis=2, tiled=True),
            lax.all_to_all(lon_items[1], "lon", split_axis=0, concat_axis=2, tiled=True),
            lax.all_to_all(lon_items[2], "lon", split_axis=0, concat_axis=2, tiled=True),
            lax.all_to_all(lon_items[3], "lon", split_axis=0, concat_axis=2, tiled=True),
        )
    )
    lon_back = side_by_side((lon_done[0], lon_done[1], lon_done[2], lon_done[3]), "lon", 2, 0, 1)
    lat_done = joint_local(
        (
            lax.all_to_all(lat_items[0], "lat", split_axis=0, concat_axis=2, tiled=True),
            lax.all_to_all(lat_items[1], "lat", split_axis=0, concat_axis=2, tiled=True),
            lax.all_to_all(lat_items[2], "lat", split_axis=0, concat_axis=2, tiled=True),
            lax.all_to_all(lat_items[3], "lat", split_axis=0, concat_axis=2, tiled=True),
        )
    )
    lat_back = side_by_side((lat_done[0], lat_done[1], lat_done[2], lat_done[3]), "lat", 2, 0, 1)
    results = []
    for lon_part, lat_part in zip(lon_back, lat_back):
        summed = lon_restore(lon_part, full_shape).astype(jnp.float32) + lat_restore(
            lat_part, full_shape
        ).astype(jnp.float32)
        results.append(summed.astype(jnp.bfloat16))
    return (results[0], results[1], results[2], results[3])


def solution(mesh):
    return jax.shard_map(
        on_device,
        mesh=mesh,
        in_specs=(
            P(None, "lat", "lon", None),
            P(None, "lat", "lon", None),
            P(None, "lat", "lon", None),
            P(None, "lat", "lon", None),
        ),
        out_specs=(
            P(None, "lat", "lon", None),
            P(None, "lat", "lon", None),
            P(None, "lat", "lon", None),
            P(None, "lat", "lon", None),
        ),
        check_vma=False,
    )
```

profile of v0, /device:TPU:1, one launch (start us, length us, event | category | flops | bytes accessed | tf_op | source)
XLA Modules:
  0.0 333.5 jit_solution(12601930708679998302)
XLA Ops:
  2.4 21.8 %all-to-all-start.5 = ((bf16[16,2,8,640]{3,2,1,0:T(8,128)(2,1)}), bf16[16,2,8,640]{3,2,1,0:T(8,128)(2,1)S(1)}, u32[]{:S(2)}, u32[]{:S(2)}) async-start(bf16[16,2,8,640]{3,2,1,0:T(8,128)(2,1)} %bitcast.24), calls=%async_computation.5 | async-start | bytes 655360 | tf_op jit(solution)/shard_map/all_to_all | solution.py:113
  25.0 18.6 %all-to-all-done.5 = bf16[16,2,8,640]{3,2,1,0:T(8,128)(2,1)S(1)} async-done(((bf16[16,2,8,640]{3,2,1,0:T(8,128)(2,1)}), bf16[16,2,8,640]{3,2,1,0:T(8,128)(2,1)S(1)}, u32[]{:S(2)}, u32[]{:S(2)}) %all-to-all-start.5) | async-done | bytes 327712 | tf_op jit(solution)/shard_map/all_to_all | solution.py:113
  43.6 3.7 %all-to-all-start.6 = ((bf16[16,2,8,640]{3,2,1,0:T(8,128)(2,1)}), bf16[16,2,8,640]{3,2,1,0:T(8,128)(2,1)S(1)}, u32[]{:S(2)}, u32[]{:S(2)}) async-start(bf16[16,2,8,640]{3,2,1,0:T(8,128)(2,1)} %bitcast.28), calls=%async_computation.6 | async-start | bytes 655360 | tf_op jit(solution)/shard_map/all_to_all | solution.py:114
  49.1 14.2 %all-to-all-done.6 = bf16[16,2,8,640]{3,2,1,0:T(8,128)(2,1)S(1)} async-done(((bf16[16,2,8,640]{3,2,1,0:T(8,128)(2,1)}), bf16[16,2,8,640]{3,2,1,0:T(8,128)(2,1)S(1)}, u32[]{:S(2)}, u32[]{:S(2)}) %all-to-all-start.6) | async-done | bytes 327712 | tf_op jit(solution)/shard_map/all_to_all | solution.py:114
  63.2 3.5 %all-to-all-start.8 = ((bf16[16,2,8,640]{3,2,1,0:T(8,128)(2,1)}), bf16[16,2,8,640]{3,2,1,0:T(8,128)(2,1)S(1)}, u32[]{:S(2)}, u32[]{:S(2)}) async-start(bf16[16,2,8,640]{3,2,1,0:T(8,128)(2,1)} %bitcast.38), calls=%async_computation.8 | async-start | bytes 655360 | tf_op jit(solution)/shard_map/all_to_all | solution.py:116
  67.8 14.9 %all-to-all-done.8 = bf16[16,2,8,640]{3,2,1,0:T(8,128)(2,1)S(1)} async-done(((bf16[16,2,8,640]{3,2,1,0:T(8,128)(2,1)}), bf16[16,2,8,640]{3,2,1,0:T(8,128)(2,1)S(1)}, u32[]{:S(2)}, u32[]{:S(2)}) %all-to-all-start.8) | async-done | bytes 327712 | tf_op jit(solution)/shard_map/all_to_all | solution.py:116
  82.7 24.6 %all_to_all.132 = bf16[16,2,8,640]{3,2,1,0:T(8,128)(2,1)S(1)} all-to-all(bf16[16,2,8,640]{3,2,1,0:T(8,128)(2,1)S(1)} %bitcast.144), channel_id=1, replica_groups=mesh['lat'=16,'lon'=64] {'lat'}, dimensions={0} | all-to-all | bytes 655360 | tf_op jit(solution)/shard_map/all_to_all | solution.py:115
  107.3 49.5 %all_to_all.133 = bf16[64,1,4,640]{3,2,1,0:T(4,128)(2,1)} all-to-all(bf16[64,1,4,640]{3,2,1,0:T(4,128)(2,1)S(1)} %bitcast.138), channel_id=1, replica_groups=mesh['lat'=16,'lon'=64] {'lon'}, dimensions={0} | all-to-all | bytes 655360 | tf_op jit(solution)/shard_map/all_to_all | solution.py:104
  156.8 19.3 %all_to_all.134 = bf16[64,1,4,640]{3,2,1,0:T(4,128)(2,1)} all-to-all(bf16[64,1,4,640]{3,2,1,0:T(4,128)(2,1)S(1)} %bitcast.139), channel_id=1, replica_groups=mesh['lat'=16,'lon'=64] {'lon'}, dimensions={0} | all-to-all | bytes 655360 | tf_op jit(solution)/shard_map/all_to_all | solution.py:105
  176.1 5.3 %all-to-all-start.2 = ((bf16[64,1,4,640]{3,2,1,0:T(4,128)(2,1)}), bf16[64,1,4,640]{3,2,1,0:T(4,128)(2,1)}, u32[]{:S(2)}, u32[]{:S(2)}) async-start(bf16[64,1,4,640]{3,2,1,0:T(4,128)(2,1)} %bitcast.2), calls=%async_computation.2 | async-start | bytes 655360 | tf_op jit(solution)/shard_map/all_to_all | solution.py:106
  187.4 8.8 %all-to-all-done.2 = bf16[64,1,4,640]{3,2,1,0:T(4,128)(2,1)} async-done(((bf16[64,1,4,640]{3,2,1,0:T(4,128)(2,1)}), bf16[64,1,4,640]{3,2,1,0:T(4,128)(2,1)}, u32[]{:S(2)}, u32[]{:S(2)}) %all-to-all-start.2) | async-done | bytes 327712 | tf_op jit(solution)/shard_map/all_to_all | solution.py:106
  196.2 5.3 %all-to-all-start.3 = ((bf16[64,1,4,640]{3,2,1,0:T(4,128)(2,1)}), bf16[64,1,4,640]{3,2,1,0:T(4,128)(2,1)}, u32[]{:S(2)}, u32[]{:S(2)}) async-start(bf16[64,1,4,640]{3,2,1,0:T(4,128)(2,1)} %bitcast.7), calls=%async_computation.3 | async-start | bytes 655360 | tf_op jit(solution)/shard_map/all_to_all | solution.py:107
  208.0 2.6 pad_maximum_fusion.1
  210.5 5.8 %all-to-all-done.3 = bf16[64,1,4,640]{3,2,1,0:T(4,128)(2,1)} async-done(((bf16[64,1,4,640]{3,2,1,0:T(4,128)(2,1)}), bf16[64,1,4,640]{3,2,1,0:T(4,128)(2,1)}, u32[]{:S(2)}, u32[]{:S(2)}) %all-to-all-start.3) | async-done | bytes 327712 | tf_op jit(solution)/shard_map/all_to_all | solution.py:107
  216.3 3.7 %all-to-all-start.9 = ((bf16[1,8,128,640]{3,1,0,2:T(8,128)(2,1)}), bf16[1,8,128,640]{3,1,0,2:T(8,128)(2,1)S(1)}, u32[]{:S(2)}, u32[]{:S(2)}) async-start(bf16[1,8,128,640]{3,1,0,2:T(8,128)(2,1)} %pad_maximum_fusion.1), calls=%async_computation.9 | async-start | bytes 2621440 | tf_op jit(solution)/shard_map/all_to_all | solution.py:12
  228.6 2.5 fusion.26
  231.1 2.5 multiply_reduce_fusion
  237.1 2.2 fusion.8
  240.8 3.0 convolution_convert_fusion.1
  245.2 3.0 convolution_convert_fusion.3
  250.2 4.9 %pad_maximum_fusion = bf16[1,4,256,640]{3,1,0,2:T(4,128)(2,1)} fusion(bf16[1,1,256,640]{3,1,0,2:T(2,128)(2,1)} %copy.88, bf16[1,1,256,640]{3,1,0,2:T(2,128)(2,1)S(1)} %copy.87, bf16[1,1,256,640]{3,1,0,2:T(2,128)(2,1)S(1)} %copy.86, bf16[1,1,256,640]{3,1,0,2:T(2,128)(2,1)S(1)} %copy.85), kind=kLoop, calls=%fused_computation.10 | loop fusion | flops 5242880 | bytes 2621440 | tf_op jit(solution)/shard_map/concatenate | solution.py:10
  255.1 28.2 %all-to-all-done.9 = bf16[1,8,128,640]{3,1,0,2:T(8,128)(2,1)S(1)} async-done(((bf16[1,8,128,640]{3,1,0,2:T(8,128)(2,1)}), bf16[1,8,128,640]{3,1,0,2:T(8,128)(2,1)S(1)}, u32[]{:S(2)}, u32[]{:S(2)}) %all-to-all-start.9) | async-done | bytes 1310752 | tf_op jit(solution)/shard_map/all_to_all | solution.py:12
  283.3 9.4 %all-to-all-start.4 = ((bf16[1,4,256,640]{3,1,0,2:T(4,128)(2,1)}), bf16[1,4,256,640]{3,1,0,2:T(4,128)(2,1)S(1)}, u32[]{:S(2)}, u32[]{:S(2)}) async-start(bf16[1,4,256,640]{3,1,0,2:T(4,128)(2,1)} %pad_maximum_fusion), calls=%async_computation.4 | async-start | bytes 2621440 | tf_op jit(solution)/shard_map/all_to_all | solution.py:12
  294.1 32.3 %all-to-all-done.4 = bf16[1,4,256,640]{3,1,0,2:T(4,128)(2,1)S(1)} async-done(((bf16[1,4,256,640]{3,1,0,2:T(4,128)(2,1)}), bf16[1,4,256,640]{3,1,0,2:T(4,128)(2,1)S(1)}, u32[]{:S(2)}, u32[]{:S(2)}) %all-to-all-start.4) | async-done | bytes 1310752 | tf_op jit(solution)/shard_map/all_to_all | solution.py:12
  (96 shorter events, 43.0 us)
Async XLA Ops:
  0.6 23.6 %copy-start.3 = (bf16[8,8,4,640]{3,2,1,0:T(4,128)(2,1)S(1)}, bf16[8,8,4,640]{3,2,1,0:T(4,128)(2,1)}, u32[]{:S(2)}) copy-start(bf16[8,8,4,640]{3,2,1,0:T(4,128)(2,1)} %param.5) | copy-start | bytes 983044
  2.4 41.2 %all-to-all-start.5 = ((bf16[16,2,8,640]{3,2,1,0:T(8,128)(2,1)}), bf16[16,2,8,640]{3,2,1,0:T(8,128)(2,1)S(1)}, u32[]{:S(2)}, u32[]{:S(2)}) async-start(bf16[16,2,8,640]{3,2,1,0:T(8,128)(2,1)} %bitcast.24), calls=%async_computation.5 | async-start | bytes 655360 | tf_op jit(solution)/shard_map/all_to_all | solution.py:113
  43.6 19.6 %all-to-all-start.6 = ((bf16[16,2,8,640]{3,2,1,0:T(8,128)(2,1)}), bf16[16,2,8,640]{3,2,1,0:T(8,128)(2,1)S(1)}, u32[]{:S(2)}, u32[]{:S(2)}) async-start(bf16[16,2,8,640]{3,2,1,0:T(8,128)(2,1)} %bitcast.28), calls=%async_computation.6 | async-start | bytes 655360 | tf_op jit(solution)/shard_map/all_to_all | solution.py:114
  47.3 60.1 %copy-start.2 = (bf16[8,8,4,640]{3,2,1,0:T(4,128)(2,1)S(1)}, bf16[8,8,4,640]{3,2,1,0:T(4,128)(2,1)}, u32[]{:S(2)}) copy-start(bf16[8,8,4,640]{3,2,1,0:T(4,128)(2,1)} %param.4) | copy-start | bytes 983044
  63.2 19.5 %all-to-all-start.8 = ((bf16[16,2,8,640]{3,2,1,0:T(8,128)(2,1)}), bf16[16,2,8,640]{3,2,1,0:T(8,128)(2,1)S(1)}, u32[]{:S(2)}, u32[]{:S(2)}) async-start(bf16[16,2,8,640]{3,2,1,0:T(8,128)(2,1)} %bitcast.38), calls=%async_computation.8 | async-start | bytes 655360 | tf_op jit(solution)/shard_map/all_to_all | solution.py:116
  176.1 20.1 %all-to-all-start.2 = ((bf16[64,1,4,640]{3,2,1,0:T(4,128)(2,1)}), bf16[64,1,4,640]{3,2,1,0:T(4,128)(2,1)}, u32[]{:S(2)}, u32[]{:S(2)}) async-start(bf16[64,1,4,640]{3,2,1,0:T(4,128)(2,1)} %bitcast.2), calls=%async_computation.2 | async-start | bytes 655360 | tf_op jit(solution)/shard_map/all_to_all | solution.py:106
  182.6 3.7 %copy-start.4 = (bf16[2,128,10,64]{1,3,2,0:T(8,128)(2,1)}, bf16[2,128,10,64]{1,3,2,0:T(8,128)(2,1)S(1)}, u32[]{:S(2)}) copy-start(bf16[2,128,10,64]{1,3,2,0:T(8,128)(2,1)S(1)} %copy.93) | copy-start | bytes 983044
  183.8 2.5 copy-start.6
  185.1 1.9 copy-start.13
  186.3 1.0 copy-start.15
  196.2 20.1 %all-to-all-start.3 = ((bf16[64,1,4,640]{3,2,1,0:T(4,128)(2,1)}), bf16[64,1,4,640]{3,2,1,0:T(4,128)(2,1)}, u32[]{:S(2)}, u32[]{:S(2)}) async-start(bf16[64,1,4,640]{3,2,1,0:T(4,128)(2,1)} %bitcast.7), calls=%async_computation.3 | async-start | bytes 655360 | tf_op jit(solution)/shard_map/all_to_all | solution.py:107
  201.5 1.0 copy-start.7
  202.5 1.0 copy-start.5
  204.7 2.0 copy-start.14
  210.5 9.5 %copy-start.9 = (bf16[64,1,4,640]{3,2,1,0:T(4,128)(2,1)S(1)}, bf16[64,1,4,640]{3,2,1,0:T(4,128)(2,1)}, u32[]{:S(2)}) copy-start(bf16[64,1,4,640]{3,2,1,0:T(4,128)(2,1)} %all_to_all.133) | copy-start | bytes 983044
  216.3 66.9 %all-to-all-start.9 = ((bf16[1,8,128,640]{3,1,0,2:T(8,128)(2,1)}), bf16[1,8,128,640]{3,1,0,2:T(8,128)(2,1)S(1)}, u32[]{:S(2)}, u32[]{:S(2)}) async-start(bf16[1,8,128,640]{3,1,0,2:T(8,128)(2,1)} %pad_maximum_fusion.1), calls=%async_computation.9 | async-start | bytes 2621440 | tf_op jit(solution)/shard_map/all_to_all | solution.py:12
  220.1 1.2 copy-start.8
  221.3 7.3 %copy-start.10 = (bf16[256,10,64]{0,2,1:T(8,128)(2,1)}, bf16[256,10,64]{0,2,1:T(8,128)(2,1)S(1)}, u32[]{:S(2)}) copy-start(bf16[256,10,64]{0,2,1:T(8,128)(2,1)S(1)} %copy.73) | copy-start | bytes 983044
  225.5 5.7 %copy-start.16 = (bf16[256,10,64]{0,2,1:T(8,128)(2,1)}, bf16[256,10,64]{0,2,1:T(8,128)(2,1)S(1)}, u32[]{:S(2)}) copy-start(bf16[256,10,64]{0,2,1:T(8,128)(2,1)S(1)} %copy.76) | copy-start | bytes 983044
  225.5 3.1 copy-start.11
  228.6 2.5 copy-start.17
  231.1 2.5 copy-start
  283.3 43.1 %all-to-all-start.4 = ((bf16[1,4,256,640]{3,1,0,2:T(4,128)(2,1)}), bf16[1,4,256,640]{3,1,0,2:T(4,128)(2,1)S(1)}, u32[]{:S(2)}, u32[]{:S(2)}) async-start(bf16[1,4,256,640]{3,1,0,2:T(4,128)(2,1)} %pad_maximum_fusion), calls=%async_computation.4 | async-start | bytes 2621440 | tf_op jit(solution)/shard_map/all_to_all | solution.py:12
  328.2 1.1 copy-start.1
  (1 other events, 1.0 us)
where the time goes:
time: 335 us; the launch traced here: 334 us
  waiting for transfers between devices  123 us (37%)
  blocking collectives  93.3 us (28%)
  starting transfers between devices  52.7 us (16%)
  local copies, waits for them, and re-layouts  35.2 us (11%)
  matrix products  18 us (5%)
  other arithmetic  10.4 us (3%)
    all_to_all x2, waiting for transfers between devices, side_by_side(): lax.all_to_all(both, axis, split_axis=split_dim, concat_axis=concat_dim,...  60.4 us
    all_to_all x1, blocking collectives, on_device(): lax.all_to_all(lon_items[0], 'lon', split_axis=0, concat_axis=2, tiled=True)  49.5 us
    all_to_all x1, blocking collectives, on_device(): lax.all_to_all(lat_items[2], 'lat', split_axis=0, concat_axis=2, tiled=True)  24.6 us
    all_to_all x1, starting transfers between devices, on_device(): lax.all_to_all(lat_items[0], 'lat', split_axis=0, concat_axis=2, tiled=True)  21.8 us
    all_to_all x1, blocking collectives, on_device(): lax.all_to_all(lon_items[1], 'lon', split_axis=0, concat_axis=2, tiled=True)  19.3 us
    all_to_all x1, waiting for transfers between devices, on_device(): lax.all_to_all(lat_items[0], 'lat', split_axis=0, concat_axis=2, tiled=True)  18.6 us
    all_to_all x1, waiting for transfers between devices, on_device(): lax.all_to_all(lat_items[3], 'lat', split_axis=0, concat_axis=2, tiled=True)  14.9 us
    all_to_all x1, waiting for transfers between devices, on_device(): lax.all_to_all(lat_items[1], 'lat', split_axis=0, concat_axis=2, tiled=True)  14.2 us
  transfers between devices with their start and end apart: 7, of which 7 were waited for; matrix products, arithmetic and copies ran while one was open for 16% of the time, Pallas kernels for 0%

commit v1 on v0

v1 whole, which is shorter than its diff:
```python
import jax
import jax.numpy as jnp
from jax import lax
from jax.experimental import pallas as pl
from jax.sharding import PartitionSpec as P


HEAD_DIM = 64
HEAD_PAIR = 2 * HEAD_DIM
FACTOR = 4


def attention_kernel(*refs):
    x_refs, o_refs = refs[: len(refs) // 2], refs[len(refs) // 2 :]
    sources, tensors, _, rows, lanes = x_refs[0].shape
    part = sources * rows
    length = part * len(x_refs)
    scale = HEAD_DIM ** (-0.5)

    def whole(t):
        parts = [r[:, t, 0].astype(jnp.float32).reshape(part, lanes) for r in x_refs]
        return jnp.concatenate(parts, axis=0).astype(jnp.bfloat16)

    q, k, v, g = (whole(t) for t in range(tensors))
    lane = lax.broadcasted_iota(jnp.int32, (length, lanes), 1)
    nt, nn, tn = ((((1,), (1,)), ((), ())), (((1,), (0,)), ((), ())), (((0,), (0,)), ((), ())))
    dot = lambda a, b, dims: lax.dot_general(a, b, dims, preferred_element_type=jnp.float32)
    totals = None
    for h in range(lanes // HEAD_DIM):
        mine = lane // HEAD_DIM == h
        qh, kh, vh, gh = (jnp.where(mine, t, jnp.zeros_like(t)) for t in (q, k, v, g))
        scores = dot(qh, kh, nt) * scale
        exps = jnp.exp(scores - jnp.max(scores, axis=-1, keepdims=True))
        probs = exps / jnp.sum(exps, axis=-1, keepdims=True)
        rounded = probs.astype(jnp.bfloat16)
        grad_probs = dot(gh, vh, nt)
        row_delta = jnp.sum(probs * grad_probs, axis=-1, keepdims=True)
        grad_scores = (probs * (grad_probs - row_delta)).astype(jnp.bfloat16)
        parts = (
            dot(rounded, vh, nn),
            dot(grad_scores, kh, nn) * scale,
            dot(grad_scores, qh, tn) * scale,
            dot(rounded, gh, tn),
        )
        totals = parts if totals is None else tuple(a + b for a, b in zip(totals, parts))
    for t in range(tensors):
        for i, r in enumerate(o_refs):
            piece = totals[t][i * part : (i + 1) * part].reshape(sources, rows, lanes)
            r[:, t, 0] = piece.astype(jnp.bfloat16)


def attention(pieces):
    sources, tensors, items, rows, feats = pieces[0].shape
    spec = pl.BlockSpec((sources, tensors, 1, rows, HEAD_PAIR), lambda i, p: (0, 0, i, 0, p))
    return pl.pallas_call(
        attention_kernel,
        grid=(items, feats // HEAD_PAIR),
        in_specs=[spec] * len(pieces),
        out_specs=[spec] * len(pieces),
        out_shape=[jax.ShapeDtypeStruct(p.shape, p.dtype) for p in pieces],
    )(*pieces)


def shift(piece, far, by):
    if by % FACTOR == 0:
        return piece
    place = lambda x, z: x * FACTOR + z
    pairs = []
    for x in range(FACTOR):
        for z in range(FACTOR):
            to = place(x, (z + by) % FACTOR) if far else place((x + by) % FACTOR, z)
            pairs.append((place(x, z), to))
    return lax.ppermute(piece, "lat", pairs)


CHUNKS = 2


def on_device(*inputs):
    batch, rows, cols, feats = inputs[0].shape
    tensors = len(inputs)
    lon = lax.axis_size("lon")
    lat = lax.axis_size("lat")
    lon_items = batch * rows // lon
    lat_items = batch * cols // lat
    me = lax.axis_index("lat")
    near, far = me // FACTOR, me % FACTOR
    swap_lon = lambda t: lax.all_to_all(t, "lon", split_axis=0, concat_axis=0, tiled=True)
    pick = lambda t, i: lax.dynamic_index_in_dim(t, i % FACTOR, 0, keepdims=False)
    part = lat_items // CHUNKS

    lon_got = swap_lon(jnp.stack([t.reshape(lon, lon_items, cols, feats) for t in inputs], axis=1))
    send = jnp.stack([t.transpose(0, 2, 1, 3).reshape(lat, lat_items, rows, feats) for t in inputs], axis=1)
    send = send.reshape((FACTOR, FACTOR) + send.shape[1:])
    far_in = []
    for c in range(CHUNKS):
        mine = send[:, :, :, c * part : (c + 1) * part]
        far_in.append([shift(pick(mine, far + k), True, k) for k in range(FACTOR)])
    (lon_done,) = attention([lon_got])
    lon_back = swap_lon(lon_done)
    home = []
    for c in range(CHUNKS):
        turned = jnp.stack(far_in[c], axis=1)
        got = [shift(pick(turned, near + m), False, m) for m in range(FACTOR)]
        done = attention(got)
        back = [shift(done[m], False, -m) for m in range(FACTOR)]
        home.append([shift(jnp.stack([b[k] for b in back], axis=0), True, -k) for k in range(FACTOR)])
    lat_back = [jnp.roll(jnp.roll(jnp.stack(h, axis=0), far, axis=0), near, axis=1) for h in home]
    lat_back = jnp.concatenate(lat_back, axis=3)
    lat_back = lat_back.reshape((lat,) + lat_back.shape[2:])
    results = []
    for i in range(tensors):
        a = lon_back[:, i].reshape(batch, rows, cols, feats)
        b = lat_back[:, i].reshape(batch, cols, rows, feats).transpose(0, 2, 1, 3)
        results.append((a.astype(jnp.float32) + b.astype(jnp.float32)).astype(jnp.bfloat16))
    return tuple(results)


def solution(mesh):
    spec = P(None, "lat", "lon", None)
    return jax.shard_map(on_device, mesh=mesh, in_specs=(spec,) * 4, out_specs=(spec,) * 4, check_vma=False)
```

time: 335 us -> 279 us (0.83)
  the two profiles are of different devices: /device:TPU:1 before, /device:TPU:75 now
where the time goes in v1:
time: 279 us; the launch traced here: 278 us
  starting transfers between devices  115 us (41%)
  waiting for transfers between devices  75.4 us (27%)
  blocking collectives  46.6 us (17%)
  Pallas kernels  21.7 us (8%)
  local copies, waits for them, and re-layouts  12.4 us (4%)
  other arithmetic  5.71 us (2%)
    ppermute x24, starting transfers between devices, shift(): return lax.ppermute(piece, 'lat', pairs)  108 us
    ppermute x24, waiting for transfers between devices, shift(): return lax.ppermute(piece, 'lat', pairs)  75.4 us
    all_to_all x1, blocking collectives, on_device(): lax.all_to_all(t, 'lon', split_axis=0, concat_axis=0, tiled=True)  46.6 us
    pallas_call x3, Pallas kernels, attention(): pl.pallas_call(attention_kernel, grid=(items, feats // HEAD_PAIR), in_spe...  21.7 us
    all_to_all x1, starting transfers between devices, on_device(): lax.all_to_all(t, 'lon', split_axis=0, concat_axis=0, tiled=True)  6.56 us
    unnamed x28, local copies, waits for them, and re-layouts  5.77 us
  transfers between devices with their start and end apart: 25, of which 4 were waited for; matrix products, arithmetic and copies ran while one was open for 3% of the time, Pallas kernels for 5%

profile of v1, /device:TPU:75, one launch (start us, length us, event | category | flops | bytes accessed | tf_op | source)
XLA Modules:
  0.0 278.2 jit_solution(5716520960157913563)
XLA Ops:
  2.9 46.6 %all_to_all.10.refs_0_ = bf16[64,4,1,4,640]{4,3,2,1,0:T(4,128)(2,1)} all-to-all(bf16[64,4,1,4,640]{4,3,2,1,0:T(4,128)(2,1)S(1)} %pad_maximum_fusion), channel_id=1, replica_groups=mesh['lat'=16,'lon'=64] {'lon'}, dimensions={0} | all-to-all | bytes 2621440 | tf_op jit(solution)/shard_map/all_to_all | solution.py:88
  49.5 8.2 %shard_map.75 = bf16[64,4,1,4,640]{4,3,2,1,0:T(4,128)(2,1)} custom-call(bf16[64,4,1,4,640]{4,3,2,1,0:T(4,128)(2,1)} %all_to_all.10.refs_0_), custom_call_target="tpu_custom_call" | custom-call | tf_op jit(solution)/shard_map/pallas_call | solution.py:55
  57.7 6.6 %all-to-all-start.1 = ((bf16[64,4,1,4,640]{4,3,2,1,0:T(4,128)(2,1)}), bf16[64,4,1,4,640]{4,3,2,1,0:T(4,128)(2,1)S(1)}, u32[]{:S(2)}, u32[]{:S(2)}) async-start(bf16[64,4,1,4,640]{4,3,2,1,0:T(4,128)(2,1)} %shard_map.75), calls=%async_computation.1 | async-start | bytes 2621440 | tf_op jit(solution)/shard_map/all_to_all | solution.py:88
  65.9 10.6 %collective-permute-start.12 = (bf16[4,4,1,8,640]{4,3,1,0,2:T(8,128)(2,1)S(1)}, bf16[4,4,1,8,640]{4,3,1,0,2:T(8,128)(2,1)S(1)}, u32[]{:S(2)}, u32[]{:S(2)}) collective-permute-start(bf16[4,4,1,8,640]{4,3,1,0,2:T(8,128)(2,1)S(1)} %bitcast.159), channel_id=1, source_target_pairs={{0,64},{64,128},{128,192},{192,0},{256,320},{320,384},{384,448},{4... | collective-permute-start | bytes 491528 | tf_op jit(solution)/shard_map/ppermute | solution.py:73
  76.6 11.6 %collective-permute-start.13 = (bf16[4,4,1,8,640]{4,3,1,0,2:T(8,128)(2,1)S(1)}, bf16[4,4,1,8,640]{4,3,1,0,2:T(8,128)(2,1)S(1)}, u32[]{:S(2)}, u32[]{:S(2)}) collective-permute-start(bf16[4,4,1,8,640]{4,3,1,0,2:T(8,128)(2,1)S(1)} %bitcast.158), channel_id=1, source_target_pairs={{0,128},{64,192},{128,0},{192,64},{256,384},{320,448},{384,256},{4... | collective-permute-start | bytes 491528 | tf_op jit(solution)/shard_map/ppermute | solution.py:73
  88.8 3.3 %collective-permute-start.14 = (bf16[4,4,1,8,640]{4,3,1,0,2:T(8,128)(2,1)}, bf16[4,4,1,8,640]{4,3,1,0,2:T(8,128)(2,1)S(1)}, u32[]{:S(2)}, u32[]{:S(2)}) collective-permute-start(bf16[4,4,1,8,640]{4,3,1,0,2:T(8,128)(2,1)} %bitcast.117), channel_id=1, source_target_pairs={{0,192},{64,0},{128,64},{192,128},{256,448},{320,256},{384,320},{4... | collective-permute-start | bytes 491528 | tf_op jit(solution)/shard_map/ppermute | solution.py:73
  92.3 5.8 %collective-permute-start = (bf16[4,4,1,8,640]{4,3,1,0,2:T(8,128)(2,1)S(1)}, bf16[4,4,1,8,640]{4,3,1,0,2:T(8,128)(2,1)S(1)}, u32[]{:S(2)}, u32[]{:S(2)}) collective-permute-start(bf16[4,4,1,8,640]{4,3,1,0,2:T(8,128)(2,1)S(1)} %bitcast.157), channel_id=1, source_target_pairs={{0,64},{64,128},{128,192},{192,0},{256,320},{320,384},{384,448},{4... | collective-permute-start | bytes 491528 | tf_op jit(solution)/shard_map/ppermute | solution.py:73
  102.1 57.5 %collective-permute-done.12 = bf16[4,4,1,8,640]{4,3,1,0,2:T(8,128)(2,1)S(1)} collective-permute-done((bf16[4,4,1,8,640]{4,3,1,0,2:T(8,128)(2,1)S(1)}, bf16[4,4,1,8,640]{4,3,1,0,2:T(8,128)(2,1)S(1)}, u32[]{:S(2)}, u32[]{:S(2)}) %collective-permute-start.12) | collective-permute-done | bytes 163872 | tf_op jit(solution)/shard_map/ppermute | solution.py:73
  159.6 3.3 %collective-permute-start.2 = (bf16[4,4,1,8,640]{4,3,1,0,2:T(8,128)(2,1)}, bf16[4,4,1,8,640]{4,3,1,0,2:T(8,128)(2,1)S(1)}, u32[]{:S(2)}, u32[]{:S(2)}) collective-permute-start(bf16[4,4,1,8,640]{4,3,1,0,2:T(8,128)(2,1)} %bitcast.121), channel_id=1, source_target_pairs={{0,192},{64,0},{128,64},{192,128},{256,448},{320,256},{384,320},{4... | collective-permute-start | bytes 491528 | tf_op jit(solution)/shard_map/ppermute | solution.py:73
  166.0 4.0 %collective-permute-start.16 = (bf16[4,4,1,8,640]{4,3,2,1,0:T(8,128)(2,1)S(1)}, bf16[4,4,1,8,640]{4,3,2,1,0:T(8,128)(2,1)S(1)}, u32[]{:S(2)}, u32[]{:S(2)}) collective-permute-start(bf16[4,4,1,8,640]{4,3,2,1,0:T(8,128)(2,1)S(1)} %get-tuple-element.49), channel_id=1, source_target_pairs={{0,512},{64,576},{128,640},{192,704},{256,768},{320,832},{384,896}... | collective-permute-start | bytes 491528 | tf_op jit(solution)/shard_map/ppermute | solution.py:73
  170.1 3.4 %collective-permute-start.15 = (bf16[4,4,1,8,640]{4,3,2,1,0:T(8,128)(2,1)S(1)}, bf16[4,4,1,8,640]{4,3,2,1,0:T(8,128)(2,1)S(1)}, u32[]{:S(2)}, u32[]{:S(2)}) collective-permute-start(bf16[4,4,1,8,640]{4,3,2,1,0:T(8,128)(2,1)S(1)} %get-tuple-element.50), channel_id=1, source_target_pairs={{0,256},{64,320},{128,384},{192,448},{256,512},{320,576},{384,640}... | collective-permute-start | bytes 491528 | tf_op jit(solution)/shard_map/ppermute | solution.py:73
  179.4 3.9 %collective-permute-start.3 = (bf16[4,4,1,8,640]{4,3,2,1,0:T(8,128)(2,1)S(1)}, bf16[4,4,1,8,640]{4,3,2,1,0:T(8,128)(2,1)S(1)}, u32[]{:S(2)}, u32[]{:S(2)}) collective-permute-start(bf16[4,4,1,8,640]{4,3,2,1,0:T(8,128)(2,1)S(1)} %get-tuple-element.42), channel_id=1, source_target_pairs={{0,256},{64,320},{128,384},{192,448},{256,512},{320,576},{384,640}... | collective-permute-start | bytes 491528 | tf_op jit(solution)/shard_map/ppermute | solution.py:73
  184.1 6.8 %shard_map.77 = (bf16[4,4,1,8,640]{4,3,2,1,0:T(8,128)(2,1)}, bf16[4,4,1,8,640]{4,3,2,1,0:T(8,128)(2,1)}, bf16[4,4,1,8,640]{4,3,2,1,0:T(8,128)(2,1)}, bf16[4,4,1,8,640]{4,3,2,1,0:T(8,128)(2,1)}) custom-call(bf16[4,4,1,8,640]{4,3,2,1,0:T(8,128)(2,1)} %get-tuple-element.51.refs_0_, bf16[4,4,1,8,640]{4,3,2,1,0:T(8,128)(2,1)} %copy-done.8, ...), custom_call_target="tpu_custom_call" | custom-call | tf_op jit(solution)/shard_map/pallas_call | solution.py:55
  191.7 3.7 %collective-permute-start.19 = (bf16[4,4,1,8,640]{4,3,1,0,2:T(8,128)(2,1)}, bf16[4,4,1,8,640]{4,3,1,0,2:T(8,128)(2,1)S(1)}, u32[]{:S(2)}, u32[]{:S(2)}) collective-permute-start(bf16[4,4,1,8,640]{4,3,1,0,2:T(8,128)(2,1)} %bitcast.167), channel_id=1, source_target_pairs={{0,512},{64,576},{128,640},{192,704},{256,768},{320,832},{384,896}... | collective-permute-start | bytes 491528 | tf_op jit(solution)/shard_map/ppermute | solution.py:73
  197.4 3.4 %collective-permute-start.20 = (bf16[4,4,1,8,640]{4,3,2,1,0:T(8,128)(2,1)}, bf16[4,4,1,8,640]{4,3,2,1,0:T(8,128)(2,1)S(1)}, u32[]{:S(2)}, u32[]{:S(2)}) collective-permute-start(bf16[4,4,1,8,640]{4,3,2,1,0:T(8,128)(2,1)} %get-tuple-element.21), channel_id=1, source_target_pairs={{0,256},{64,320},{128,384},{192,448},{256,512},{320,576},{384,640}... | collective-permute-start | bytes 491528 | tf_op jit(solution)/shard_map/ppermute | solution.py:73
  201.5 6.8 %shard_map.76 = (bf16[4,4,1,8,640]{4,3,2,1,0:T(8,128)(2,1)}, bf16[4,4,1,8,640]{4,3,2,1,0:T(8,128)(2,1)}, bf16[4,4,1,8,640]{4,3,2,1,0:T(8,128)(2,1)}, bf16[4,4,1,8,640]{4,3,2,1,0:T(8,128)(2,1)}) custom-call(bf16[4,4,1,8,640]{4,3,2,1,0:T(8,128)(2,1)} %get-tuple-element.43.refs_0_, bf16[4,4,1,8,640]{4,3,2,1,0:T(8,128)(2,1)} %copy-done.9, ...), custom_call_target="tpu_custom_call" | custom-call | tf_op jit(solution)/shard_map/pallas_call | solution.py:55
  210.7 3.7 %collective-permute-start.7 = (bf16[4,4,1,8,640]{4,3,1,0,2:T(8,128)(2,1)}, bf16[4,4,1,8,640]{4,3,1,0,2:T(8,128)(2,1)S(1)}, u32[]{:S(2)}, u32[]{:S(2)}) collective-permute-start(bf16[4,4,1,8,640]{4,3,1,0,2:T(8,128)(2,1)} %bitcast.164), channel_id=1, source_target_pairs={{0,512},{64,576},{128,640},{192,704},{256,768},{320,832},{384,896}... | collective-permute-start | bytes 491528 | tf_op jit(solution)/shard_map/ppermute | solution.py:73
  216.1 4.0 %collective-permute-start.8 = (bf16[4,4,1,8,640]{4,3,1,0,2:T(8,128)(2,1)}, bf16[4,4,1,8,640]{4,3,1,0,2:T(8,128)(2,1)S(1)}, u32[]{:S(2)}, u32[]{:S(2)}) collective-permute-start(bf16[4,4,1,8,640]{4,3,1,0,2:T(8,128)(2,1)} %bitcast.163), channel_id=1, source_target_pairs={{0,256},{64,320},{128,384},{192,448},{256,512},{320,576},{384,640}... | collective-permute-start | bytes 491528 | tf_op jit(solution)/shard_map/ppermute | solution.py:73
  222.2 10.9 %collective-permute-start.22 = (bf16[4,4,1,8,640]{4,3,1,0,2:T(8,128)(2,1)S(1)}, bf16[4,4,1,8,640]{4,3,1,0,2:T(8,128)(2,1)S(1)}, u32[]{:S(2)}, u32[]{:S(2)}) collective-permute-start(bf16[4,4,1,8,640]{4,3,1,0,2:T(8,128)(2,1)S(1)} %pad_maximum_fusion.9), channel_id=1, source_target_pairs={{0,128},{64,192},{128,0},{192,64},{256,384},{320,448},{384,256},{4... | collective-permute-start | bytes 491528 | tf_op jit(solution)/shard_map/ppermute | solution.py:73
  235.2 7.3 %collective-permute-start.9 = (bf16[4,4,1,8,640]{4,3,1,0,2:T(8,128)(2,1)S(1)}, bf16[4,4,1,8,640]{4,3,1,0,2:T(8,128)(2,1)S(1)}, u32[]{:S(2)}, u32[]{:S(2)}) collective-permute-start(bf16[4,4,1,8,640]{4,3,1,0,2:T(8,128)(2,1)S(1)} %pad_maximum_fusion.5), channel_id=1, source_target_pairs={{0,192},{64,0},{128,64},{192,128},{256,448},{320,256},{384,320},{4... | collective-permute-start | bytes 491528 | tf_op jit(solution)/shard_map/ppermute | solution.py:73
  242.5 3.1 %collective-permute-start.10 = (bf16[4,4,1,8,640]{4,3,1,0,2:T(8,128)(2,1)S(1)}, bf16[4,4,1,8,640]{4,3,1,0,2:T(8,128)(2,1)S(1)}, u32[]{:S(2)}, u32[]{:S(2)}) collective-permute-start(bf16[4,4,1,8,640]{4,3,1,0,2:T(8,128)(2,1)S(1)} %pad_maximum_fusion.6), channel_id=1, source_target_pairs={{0,128},{64,192},{128,0},{192,64},{256,384},{320,448},{384,256},{4... | collective-permute-start | bytes 491528 | tf_op jit(solution)/shard_map/ppermute | solution.py:73
  245.8 7.4 %collective-permute-start.11 = (bf16[4,4,1,8,640]{4,3,1,0,2:T(8,128)(2,1)S(1)}, bf16[4,4,1,8,640]{4,3,1,0,2:T(8,128)(2,1)S(1)}, u32[]{:S(2)}, u32[]{:S(2)}) collective-permute-start(bf16[4,4,1,8,640]{4,3,1,0,2:T(8,128)(2,1)S(1)} %pad_maximum_fusion.7), channel_id=1, source_target_pairs={{0,64},{64,128},{128,192},{192,0},{256,320},{320,384},{384,448},{4... | collective-permute-start | bytes 491528 | tf_op jit(solution)/shard_map/ppermute | solution.py:73
  254.3 7.6 %collective-permute-done.10 = bf16[4,4,1,8,640]{4,3,1,0,2:T(8,128)(2,1)S(1)} collective-permute-done((bf16[4,4,1,8,640]{4,3,1,0,2:T(8,128)(2,1)S(1)}, bf16[4,4,1,8,640]{4,3,1,0,2:T(8,128)(2,1)S(1)}, u32[]{:S(2)}, u32[]{:S(2)}) %collective-permute-start.10) | collective-permute-done | bytes 163872 | tf_op jit(solution)/shard_map/ppermute | solution.py:73
  261.8 10.1 %collective-permute-done.11 = bf16[4,4,1,8,640]{4,3,1,0,2:T(8,128)(2,1)S(1)} collective-permute-done((bf16[4,4,1,8,640]{4,3,1,0,2:T(8,128)(2,1)S(1)}, bf16[4,4,1,8,640]{4,3,1,0,2:T(8,128)(2,1)S(1)}, u32[]{:S(2)}, u32[]{:S(2)}) %collective-permute-start.11) | collective-permute-done | bytes 163872 | tf_op jit(solution)/shard_map/ppermute | solution.py:73
  (108 shorter events, 36.9 us)
Async XLA Ops:
  57.7 216.0 %all-to-all-start.1 = ((bf16[64,4,1,4,640]{4,3,2,1,0:T(4,128)(2,1)}), bf16[64,4,1,4,640]{4,3,2,1,0:T(4,128)(2,1)S(1)}, u32[]{:S(2)}, u32[]{:S(2)}) async-start(bf16[64,4,1,4,640]{4,3,2,1,0:T(4,128)(2,1)} %shard_map.75), calls=%async_computation.1 | async-start | bytes 2621440 | tf_op jit(solution)/shard_map/all_to_all | solution.py:88
  65.9 93.7 %collective-permute-start.12 = (bf16[4,4,1,8,640]{4,3,1,0,2:T(8,128)(2,1)S(1)}, bf16[4,4,1,8,640]{4,3,1,0,2:T(8,128)(2,1)S(1)}, u32[]{:S(2)}, u32[]{:S(2)}) collective-permute-start(bf16[4,4,1,8,640]{4,3,1,0,2:T(8,128)(2,1)S(1)} %bitcast.159), channel_id=1, source_target_pairs={{0,64},{64,128},{128,192},{192,0},{256,320},{320,384},{384,448},{4... | collective-permute-start | bytes 491528 | tf_op jit(solution)/shard_map/ppermute | solution.py:73
  76.6 86.4 %collective-permute-start.13 = (bf16[4,4,1,8,640]{4,3,1,0,2:T(8,128)(2,1)S(1)}, bf16[4,4,1,8,640]{4,3,1,0,2:T(8,128)(2,1)S(1)}, u32[]{:S(2)}, u32[]{:S(2)}) collective-permute-start(bf16[4,4,1,8,640]{4,3,1,0,2:T(8,128)(2,1)S(1)} %bitcast.158), channel_id=1, source_target_pairs={{0,128},{64,192},{128,0},{192,64},{256,384},{320,448},{384,256},{4... | collective-permute-start | bytes 491528 | tf_op jit(solution)/shard_map/ppermute | solution.py:73
  88.8 74.1 %collective-permute-start.14 = (bf16[4,4,1,8,640]{4,3,1,0,2:T(8,128)(2,1)}, bf16[4,4,1,8,640]{4,3,1,0,2:T(8,128)(2,1)S(1)}, u32[]{:S(2)}, u32[]{:S(2)}) collective-permute-start(bf16[4,4,1,8,640]{4,3,1,0,2:T(8,128)(2,1)} %bitcast.117), channel_id=1, source_target_pairs={{0,192},{64,0},{128,64},{192,128},{256,448},{320,256},{384,320},{4... | collective-permute-start | bytes 491528 | tf_op jit(solution)/shard_map/ppermute | solution.py:73
  92.3 77.8 %collective-permute-start = (bf16[4,4,1,8,640]{4,3,1,0,2:T(8,128)(2,1)S(1)}, bf16[4,4,1,8,640]{4,3,1,0,2:T(8,128)(2,1)S(1)}, u32[]{:S(2)}, u32[]{:S(2)}) collective-permute-start(bf16[4,4,1,8,640]{4,3,1,0,2:T(8,128)(2,1)S(1)} %bitcast.157), channel_id=1, source_target_pairs={{0,64},{64,128},{128,192},{192,0},{256,320},{320,384},{384,448},{4... | collective-permute-start | bytes 491528 | tf_op jit(solution)/shard_map/ppermute | solution.py:73
  98.2 75.3 %collective-permute-start.1 = (bf16[4,4,1,8,640]{4,3,1,0,2:T(8,128)(2,1)S(1)}, bf16[4,4,1,8,640]{4,3,1,0,2:T(8,128)(2,1)S(1)}, u32[]{:S(2)}, u32[]{:S(2)}) collective-permute-start(bf16[4,4,1,8,640]{4,3,1,0,2:T(8,128)(2,1)S(1)} %bitcast.156), channel_id=1, source_target_pairs={{0,128},{64,192},{128,0},{192,64},{256,384},{320,448},{384,256},{4... | collective-permute-start | bytes 491528 | tf_op jit(solution)/shard_map/ppermute | solution.py:73
  159.6 13.9 %collective-permute-start.2 = (bf16[4,4,1,8,640]{4,3,1,0,2:T(8,128)(2,1)}, bf16[4,4,1,8,640]{4,3,1,0,2:T(8,128)(2,1)S(1)}, u32[]{:S(2)}, u32[]{:S(2)}) collective-permute-start(bf16[4,4,1,8,640]{4,3,1,0,2:T(8,128)(2,1)} %bitcast.121), channel_id=1, source_target_pairs={{0,192},{64,0},{128,64},{192,128},{256,448},{320,256},{384,320},{4... | collective-permute-start | bytes 491528 | tf_op jit(solution)/shard_map/ppermute | solution.py:73
  163.9 15.6 %collective-permute-start.17 = (bf16[4,4,1,8,640]{4,3,2,1,0:T(8,128)(2,1)S(1)}, bf16[4,4,1,8,640]{4,3,2,1,0:T(8,128)(2,1)S(1)}, u32[]{:S(2)}, u32[]{:S(2)}) collective-permute-start(bf16[4,4,1,8,640]{4,3,2,1,0:T(8,128)(2,1)S(1)} %get-tuple-element.48), channel_id=1, source_target_pairs={{0,768},{64,832},{128,896},{192,960},{256,0},{320,64},{384,128},{4... | collective-permute-start | bytes 491528 | tf_op jit(solution)/shard_map/ppermute | solution.py:73
  166.0 17.4 %collective-permute-start.16 = (bf16[4,4,1,8,640]{4,3,2,1,0:T(8,128)(2,1)S(1)}, bf16[4,4,1,8,640]{4,3,2,1,0:T(8,128)(2,1)S(1)}, u32[]{:S(2)}, u32[]{:S(2)}) collective-permute-start(bf16[4,4,1,8,640]{4,3,2,1,0:T(8,128)(2,1)S(1)} %get-tuple-element.49), channel_id=1, source_target_pairs={{0,512},{64,576},{128,640},{192,704},{256,768},{320,832},{384,896}... | collective-permute-start | bytes 491528 | tf_op jit(solution)/shard_map/ppermute | solution.py:73
  174.4 22.9 %collective-permute-start.5 = (bf16[4,4,1,8,640]{4,3,2,1,0:T(8,128)(2,1)S(1)}, bf16[4,4,1,8,640]{4,3,2,1,0:T(8,128)(2,1)S(1)}, u32[]{:S(2)}, u32[]{:S(2)}) collective-permute-start(bf16[4,4,1,8,640]{4,3,2,1,0:T(8,128)(2,1)S(1)} %get-tuple-element.40), channel_id=1, source_target_pairs={{0,768},{64,832},{128,896},{192,960},{256,0},{320,64},{384,128},{4... | collective-permute-start | bytes 491528 | tf_op jit(solution)/shard_map/ppermute | solution.py:73
  176.3 24.4 %collective-permute-start.4 = (bf16[4,4,1,8,640]{4,3,2,1,0:T(8,128)(2,1)S(1)}, bf16[4,4,1,8,640]{4,3,2,1,0:T(8,128)(2,1)S(1)}, u32[]{:S(2)}, u32[]{:S(2)}) collective-permute-start(bf16[4,4,1,8,640]{4,3,2,1,0:T(8,128)(2,1)S(1)} %get-tuple-element.41), channel_id=1, source_target_pairs={{0,512},{64,576},{128,640},{192,704},{256,768},{320,832},{384,896}... | collective-permute-start | bytes 491528 | tf_op jit(solution)/shard_map/ppermute | solution.py:73
  179.4 21.3 %collective-permute-start.3 = (bf16[4,4,1,8,640]{4,3,2,1,0:T(8,128)(2,1)S(1)}, bf16[4,4,1,8,640]{4,3,2,1,0:T(8,128)(2,1)S(1)}, u32[]{:S(2)}, u32[]{:S(2)}) collective-permute-start(bf16[4,4,1,8,640]{4,3,2,1,0:T(8,128)(2,1)S(1)} %get-tuple-element.42), channel_id=1, source_target_pairs={{0,256},{64,320},{128,384},{192,448},{256,512},{320,576},{384,640}... | collective-permute-start | bytes 491528 | tf_op jit(solution)/shard_map/ppermute | solution.py:73
  191.7 24.4 %collective-permute-start.19 = (bf16[4,4,1,8,640]{4,3,1,0,2:T(8,128)(2,1)}, bf16[4,4,1,8,640]{4,3,1,0,2:T(8,128)(2,1)S(1)}, u32[]{:S(2)}, u32[]{:S(2)}) collective-permute-start(bf16[4,4,1,8,640]{4,3,1,0,2:T(8,128)(2,1)} %bitcast.167), channel_id=1, source_target_pairs={{0,512},{64,576},{128,640},{192,704},{256,768},{320,832},{384,896}... | collective-permute-start | bytes 491528 | tf_op jit(solution)/shard_map/ppermute | solution.py:73
  195.4 24.7 %collective-permute-start.18 = (bf16[4,4,1,8,640]{4,3,1,0,2:T(8,128)(2,1)}, bf16[4,4,1,8,640]{4,3,1,0,2:T(8,128)(2,1)S(1)}, u32[]{:S(2)}, u32[]{:S(2)}) collective-permute-start(bf16[4,4,1,8,640]{4,3,1,0,2:T(8,128)(2,1)} %bitcast.166), channel_id=1, source_target_pairs={{0,768},{64,832},{128,896},{192,960},{256,0},{320,64},{384,128},{4... | collective-permute-start | bytes 491528 | tf_op jit(solution)/shard_map/ppermute | solution.py:73
  197.4 22.7 %collective-permute-start.20 = (bf16[4,4,1,8,640]{4,3,2,1,0:T(8,128)(2,1)}, bf16[4,4,1,8,640]{4,3,2,1,0:T(8,128)(2,1)S(1)}, u32[]{:S(2)}, u32[]{:S(2)}) collective-permute-start(bf16[4,4,1,8,640]{4,3,2,1,0:T(8,128)(2,1)} %get-tuple-element.21), channel_id=1, source_target_pairs={{0,256},{64,320},{128,384},{192,448},{256,512},{320,576},{384,640}... | collective-permute-start | bytes 491528 | tf_op jit(solution)/shard_map/ppermute | solution.py:73
  208.2 24.9 %collective-permute-start.6 = (bf16[4,4,1,8,640]{4,3,1,0,2:T(8,128)(2,1)}, bf16[4,4,1,8,640]{4,3,1,0,2:T(8,128)(2,1)S(1)}, u32[]{:S(2)}, u32[]{:S(2)}) collective-permute-start(bf16[4,4,1,8,640]{4,3,1,0,2:T(8,128)(2,1)} %bitcast.165), channel_id=1, source_target_pairs={{0,768},{64,832},{128,896},{192,960},{256,0},{320,64},{384,128},{4... | collective-permute-start | bytes 491528 | tf_op jit(solution)/shard_map/ppermute | solution.py:73
  210.7 24.4 %collective-permute-start.7 = (bf16[4,4,1,8,640]{4,3,1,0,2:T(8,128)(2,1)}, bf16[4,4,1,8,640]{4,3,1,0,2:T(8,128)(2,1)S(1)}, u32[]{:S(2)}, u32[]{:S(2)}) collective-permute-start(bf16[4,4,1,8,640]{4,3,1,0,2:T(8,128)(2,1)} %bitcast.164), channel_id=1, source_target_pairs={{0,512},{64,576},{128,640},{192,704},{256,768},{320,832},{384,896}... | collective-permute-start | bytes 491528 | tf_op jit(solution)/shard_map/ppermute | solution.py:73
  216.1 19.0 %collective-permute-start.8 = (bf16[4,4,1,8,640]{4,3,1,0,2:T(8,128)(2,1)}, bf16[4,4,1,8,640]{4,3,1,0,2:T(8,128)(2,1)S(1)}, u32[]{:S(2)}, u32[]{:S(2)}) collective-permute-start(bf16[4,4,1,8,640]{4,3,1,0,2:T(8,128)(2,1)} %bitcast.163), channel_id=1, source_target_pairs={{0,256},{64,320},{128,384},{192,448},{256,512},{320,576},{384,640}... | collective-permute-start | bytes 491528 | tf_op jit(solution)/shard_map/ppermute | solution.py:73
  220.2 25.5 %collective-permute-start.21 = (bf16[4,4,1,8,640]{4,3,1,0,2:T(8,128)(2,1)S(1)}, bf16[4,4,1,8,640]{4,3,1,0,2:T(8,128)(2,1)S(1)}, u32[]{:S(2)}, u32[]{:S(2)}) collective-permute-start(bf16[4,4,1,8,640]{4,3,1,0,2:T(8,128)(2,1)S(1)} %pad_maximum_fusion.8), channel_id=1, source_target_pairs={{0,192},{64,0},{128,64},{192,128},{256,448},{320,256},{384,320},{4... | collective-permute-start | bytes 491528 | tf_op jit(solution)/shard_map/ppermute | solution.py:73
  222.2 31.0 %collective-permute-start.22 = (bf16[4,4,1,8,640]{4,3,1,0,2:T(8,128)(2,1)S(1)}, bf16[4,4,1,8,640]{4,3,1,0,2:T(8,128)(2,1)S(1)}, u32[]{:S(2)}, u32[]{:S(2)}) collective-permute-start(bf16[4,4,1,8,640]{4,3,1,0,2:T(8,128)(2,1)S(1)} %pad_maximum_fusion.9), channel_id=1, source_target_pairs={{0,128},{64,192},{128,0},{192,64},{256,384},{320,448},{384,256},{4... | collective-permute-start | bytes 491528 | tf_op jit(solution)/shard_map/ppermute | solution.py:73
  233.2 20.1 %collective-permute-start.23 = (bf16[4,4,1,8,640]{4,3,2,1,0:T(8,128)(2,1)S(1)}, bf16[4,4,1,8,640]{4,3,2,1,0:T(8,128)(2,1)S(1)}, u32[]{:S(2)}, u32[]{:S(2)}) collective-permute-start(bf16[4,4,1,8,640]{4,3,2,1,0:T(8,128)(2,1)S(1)} %pad_maximum_fusion.10), channel_id=1, source_target_pairs={{0,64},{64,128},{128,192},{192,0},{256,320},{320,384},{384,448},{4... | collective-permute-start | bytes 491528 | tf_op jit(solution)/shard_map/ppermute | solution.py:73
  235.2 19.1 %collective-permute-start.9 = (bf16[4,4,1,8,640]{4,3,1,0,2:T(8,128)(2,1)S(1)}, bf16[4,4,1,8,640]{4,3,1,0,2:T(8,128)(2,1)S(1)}, u32[]{:S(2)}, u32[]{:S(2)}) collective-permute-start(bf16[4,4,1,8,640]{4,3,1,0,2:T(8,128)(2,1)S(1)} %pad_maximum_fusion.5), channel_id=1, source_target_pairs={{0,192},{64,0},{128,64},{192,128},{256,448},{320,256},{384,320},{4... | collective-permute-start | bytes 491528 | tf_op jit(solution)/shard_map/ppermute | solution.py:73
  242.5 19.3 %collective-permute-start.10 = (bf16[4,4,1,8,640]{4,3,1,0,2:T(8,128)(2,1)S(1)}, bf16[4,4,1,8,640]{4,3,1,0,2:T(8,128)(2,1)S(1)}, u32[]{:S(2)}, u32[]{:S(2)}) collective-permute-start(bf16[4,4,1,8,640]{4,3,1,0,2:T(8,128)(2,1)S(1)} %pad_maximum_fusion.6), channel_id=1, source_target_pairs={{0,128},{64,192},{128,0},{192,64},{256,384},{320,448},{384,256},{4... | collective-permute-start | bytes 491528 | tf_op jit(solution)/shard_map/ppermute | solution.py:73
  245.8 26.2 %collective-permute-start.11 = (bf16[4,4,1,8,640]{4,3,1,0,2:T(8,128)(2,1)S(1)}, bf16[4,4,1,8,640]{4,3,1,0,2:T(8,128)(2,1)S(1)}, u32[]{:S(2)}, u32[]{:S(2)}) collective-permute-start(bf16[4,4,1,8,640]{4,3,1,0,2:T(8,128)(2,1)S(1)} %pad_maximum_fusion.7), channel_id=1, source_target_pairs={{0,64},{64,128},{128,192},{192,0},{256,320},{320,384},{384,448},{4... | collective-permute-start | bytes 491528 | tf_op jit(solution)/shard_map/ppermute | solution.py:73
  (11 other events, 38.9 us)

commit v2 on v1

v2 whole, which is shorter than its diff:
```python
import jax
import jax.numpy as jnp
from jax import lax
from jax.experimental import pallas as pl
from jax.experimental.pallas import tpu as pltpu
from jax.sharding import PartitionSpec as P


HEAD_DIM = 64
HEAD_PAIR = 2 * HEAD_DIM
FACTOR = 4
CHUNKS = 2


def attend(x_refs, o_refs, item, lanes):
    sources, tensors, _, rows, _ = x_refs[0].shape
    part = sources * rows
    length = part * len(x_refs)
    scale = HEAD_DIM ** (-0.5)
    full_tiles = rows % 8 == 0

    def whole(t):
        if full_tiles:
            return jnp.concatenate([r[:, t, item, :, lanes].reshape(part, HEAD_PAIR) for r in x_refs], axis=0)
        parts = [r[:, t, item, :, lanes].astype(jnp.float32).reshape(part, HEAD_PAIR) for r in x_refs]
        return jnp.concatenate(parts, axis=0).astype(jnp.bfloat16)

    q, k, v, g = (whole(t) for t in range(tensors))
    lane = lax.broadcasted_iota(jnp.int32, (length, HEAD_PAIR), 1)
    nt, nn, tn = ((((1,), (1,)), ((), ())), (((1,), (0,)), ((), ())), (((0,), (0,)), ((), ())))
    dot = lambda a, b, dims: lax.dot_general(a, b, dims, preferred_element_type=jnp.float32)
    totals = None
    for h in range(HEAD_PAIR // HEAD_DIM):
        mine = lane // HEAD_DIM == h
        qh, kh, vh, gh = (jnp.where(mine, t, jnp.zeros_like(t)) for t in (q, k, v, g))
        scores = dot(qh, k, nt) * scale
        exps = jnp.exp(scores - jnp.max(scores, axis=-1, keepdims=True))
        probs = exps * (1.0 / jnp.sum(exps, axis=-1, keepdims=True))
        rounded = probs.astype(jnp.bfloat16)
        grad_probs = dot(gh, v, nt)
        row_delta = jnp.sum(probs * grad_probs, axis=-1, keepdims=True)
        grad_scores = (probs * (grad_probs - row_delta)).astype(jnp.bfloat16)
        parts = (dot(rounded, vh, nn), dot(grad_scores, kh, nn), dot(grad_scores, qh, tn), dot(rounded, gh, tn))
        totals = parts if totals is None else tuple(a + b for a, b in zip(totals, parts))
    totals = (totals[0], totals[1] * scale, totals[2] * scale, totals[3])
    for t in range(tensors):
        done = totals[t].astype(jnp.bfloat16) if full_tiles else totals[t]
        for i, r in enumerate(o_refs):
            piece = done[i * part : (i + 1) * part].reshape(sources, rows, HEAD_PAIR)
            r[:, t, item, :, lanes] = piece.astype(jnp.bfloat16)


def attention_kernel(*refs):
    x_refs, o_refs = refs[: len(refs) // 2], refs[len(refs) // 2 :]
    items, feats = x_refs[0].shape[2], x_refs[0].shape[4]
    for item in range(items):
        for pair in range(feats // HEAD_PAIR):
            attend(x_refs, o_refs, item, pl.ds(pair * HEAD_PAIR, HEAD_PAIR))


def attention(pieces):
    spec = pl.BlockSpec(memory_space=pltpu.VMEM)
    return pl.pallas_call(
        attention_kernel,
        in_specs=[spec] * len(pieces),
        out_specs=[spec] * len(pieces),
        out_shape=[jax.ShapeDtypeStruct(p.shape, p.dtype) for p in pieces],
    )(*pieces)


def shift(piece, far, by):
    if by % FACTOR == 0:
        return piece
    place = lambda x, z: x * FACTOR + z
    pairs = []
    for x in range(FACTOR):
        for z in range(FACTOR):
            to = place(x, (z + by) % FACTOR) if far else place((x + by) % FACTOR, z)
            pairs.append((place(x, z), to))
    return lax.ppermute(piece, "lat", pairs)


def on_device(*inputs):
    batch, rows, cols, feats = inputs[0].shape
    tensors = len(inputs)
    lon = lax.axis_size("lon")
    lat = lax.axis_size("lat")
    lon_items = batch * rows // lon
    lat_items = batch * cols // lat
    part = lat_items // CHUNKS
    me = lax.axis_index("lat")
    near, far = me // FACTOR, me % FACTOR
    swap_lon = lambda t: lax.all_to_all(t, "lon", split_axis=0, concat_axis=0, tiled=True)
    pick = lambda t, i: lax.dynamic_index_in_dim(t, i % FACTOR, 0, keepdims=False)

    lon_got = swap_lon(jnp.stack([t.reshape(lon, lon_items, cols, feats) for t in inputs], axis=1))
    send = jnp.stack([t.transpose(0, 2, 1, 3).reshape(lat, lat_items, rows, feats) for t in inputs], axis=1)
    send = send.reshape((FACTOR, FACTOR) + send.shape[1:])
    turned = jnp.stack([shift(pick(send, near + m), False, m) for m in range(FACTOR)], axis=1)
    home = []
    for c in range(CHUNKS):
        mine = turned[:, :, :, c * part : (c + 1) * part]
        got = [shift(pick(mine, far + k), True, k) for k in range(FACTOR)]
        done = attention(got)
        home.append([shift(done[k], True, -k) for k in range(FACTOR)])
    (lon_done,) = attention([lon_got])
    lon_back = swap_lon(lon_done)
    joined = [jnp.concatenate([h[k] for h in home], axis=2) for k in range(FACTOR)]
    back = [shift(jnp.stack([j[m] for j in joined], axis=0), False, -m) for m in range(FACTOR)]
    lat_back = jnp.roll(jnp.roll(jnp.stack(back, axis=0), near, axis=0), far, axis=1)
    lat_back = lat_back.reshape((lat,) + lat_back.shape[2:])
    results = []
    for i in range(tensors):
        a = lon_back[:, i].reshape(batch, rows, cols, feats)
        b = lat_back[:, i].reshape(batch, cols, rows, feats).transpose(0, 2, 1, 3)
        results.append((a.astype(jnp.float32) + b.astype(jnp.float32)).astype(jnp.bfloat16))
    return tuple(results)


def solution(mesh):
    spec = P(None, "lat", "lon", None)
    return jax.shard_map(on_device, mesh=mesh, in_specs=(spec,) * 4, out_specs=(spec,) * 4, check_vma=False)
```

time: 279 us -> 271 us (0.971)
  the two profiles are of different devices: /device:TPU:75 before, /device:TPU:128 now
where the time goes in v2:
time: 271 us; the launch traced here: 270 us
  starting transfers between devices  147 us (54%)
  waiting for transfers between devices  87 us (32%)
  Pallas kernels  16.3 us (6%)
  local copies, waits for them, and re-layouts  11.9 us (4%)
  other arithmetic  6.12 us (2%)
    ppermute x18, starting transfers between devices, shift(): return lax.ppermute(piece, 'lat', pairs)  125 us
    ppermute x18, waiting for transfers between devices, shift(): return lax.ppermute(piece, 'lat', pairs)  78.3 us
    all_to_all x2, starting transfers between devices, on_device(): lax.all_to_all(t, 'lon', split_axis=0, concat_axis=0, tiled=True)  21.9 us
    pallas_call x3, Pallas kernels, attention(): pl.pallas_call(attention_kernel, in_specs=[spec] * len(pieces), out_specs...  16.3 us
    all_to_all x2, waiting for transfers between devices, on_device(): lax.all_to_all(t, 'lon', split_axis=0, concat_axis=0, tiled=True)  8.71 us
    unnamed x47, local copies, waits for them, and re-layouts  8.1 us
  transfers between devices with their start and end apart: 20, of which 9 were waited for; matrix products, arithmetic and copies ran while one was open for 3% of the time, Pallas kernels for 4%

profile of v2, /device:TPU:128, one launch (start us, length us, event | category | flops | bytes accessed | tf_op | source)
XLA Modules:
  0.0 270.2 jit_solution(13738744693305144956)
XLA Ops:
  0.6 3.4 %pad_maximum_fusion = bf16[64,4,1,4,640]{4,3,2,1,0:T(4,128)(2,1)} fusion(bf16[64,1,1,4,640]{4,3,2,1,0:T(4,128)(2,1)} %bitcast.109, bf16[64,1,1,4,640]{4,3,2,1,0:T(4,128)(2,1)} %bitcast.108, bf16[64,1,1,4,640]{4,3,2,1,0:T(4,128)(2,1)} %bitcast.111, bf16[64,1,1,4,640]{4,3,2,1,0:T(4,128)(2,1)} %bitcast.110), kind=kLoop, calls=%fused_computation.3 | loop fusion | flops 1966080 | bytes 2621440 | tf_op jit(solution)/shard_map/stack | solution.py:96
  4.0 15.6 %all-to-all-start = ((bf16[64,4,1,4,640]{4,3,2,1,0:T(4,128)(2,1)}), bf16[64,4,1,4,640]{4,3,2,1,0:T(4,128)(2,1)S(1)}, u32[]{:S(2)}, u32[]{:S(2)}) async-start(bf16[64,4,1,4,640]{4,3,2,1,0:T(4,128)(2,1)} %pad_maximum_fusion), calls=%async_computation | async-start | bytes 2621440 | tf_op jit(solution)/shard_map/all_to_all | solution.py:93
  25.6 4.6 %collective-permute-start.2 = (bf16[4,4,2,8,640]{4,3,2,1,0:T(8,128)(2,1)S(1)}, bf16[4,4,2,8,640]{4,3,2,1,0:T(8,128)(2,1)}, u32[]{:S(2)}, u32[]{:S(2)}) collective-permute-start(bf16[4,4,2,8,640]{4,3,2,1,0:T(8,128)(2,1)S(1)} %bitcast.124), channel_id=1, source_target_pairs={{0,768},{64,832},{128,896},{192,960},{256,0},{320,64},{384,128},{4... | collective-permute-start | bytes 983048 | tf_op jit(solution)/shard_map/ppermute | solution.py:80
  30.4 10.6 %collective-permute-done = bf16[4,4,2,8,640]{4,3,2,1,0:T(8,128)(2,1)S(1)} collective-permute-done((bf16[4,4,2,8,640]{4,3,2,1,0:T(8,128)(2,1)S(1)}, bf16[4,4,2,8,640]{4,3,2,1,0:T(8,128)(2,1)S(1)}, u32[]{:S(2)}, u32[]{:S(2)}) %collective-permute-start) | collective-permute-done | bytes 327712 | tf_op jit(solution)/shard_map/ppermute | solution.py:80
  41.0 2.7 collective-permute-done.2
  45.0 8.7 %all-to-all-done.refs_0_ = bf16[64,4,1,4,640]{4,3,2,1,0:T(4,128)(2,1)S(1)} async-done(((bf16[64,4,1,4,640]{4,3,2,1,0:T(4,128)(2,1)}), bf16[64,4,1,4,640]{4,3,2,1,0:T(4,128)(2,1)S(1)}, u32[]{:S(2)}, u32[]{:S(2)}) %all-to-all-start) | async-done | bytes 1310752 | tf_op jit(solution)/shard_map/all_to_all | solution.py:93
  54.7 6.6 %shard_map.75 = bf16[64,4,1,4,640]{4,3,2,1,0:T(4,128)(2,1)} custom-call(bf16[64,4,1,4,640]{4,3,2,1,0:T(4,128)(2,1)} %copy-done), custom_call_target="tpu_custom_call" | custom-call | tf_op jit(solution)/shard_map/pallas_call | solution.py:63
  61.3 6.3 %all-to-all-start.1 = ((bf16[64,4,1,4,640]{4,3,2,1,0:T(4,128)(2,1)}), bf16[64,4,1,4,640]{4,3,2,1,0:T(4,128)(2,1)S(1)}, u32[]{:S(2)}, u32[]{:S(2)}) async-start(bf16[64,4,1,4,640]{4,3,2,1,0:T(4,128)(2,1)} %shard_map.75), calls=%async_computation.1 | async-start | bytes 2621440 | tf_op jit(solution)/shard_map/all_to_all | solution.py:93
  68.5 7.2 %collective-permute-start.3 = (bf16[4,4,1,8,640]{4,3,2,1,0:T(8,128)(2,1)S(1)}, bf16[4,4,1,8,640]{4,3,2,1,0:T(8,128)(2,1)S(1)}, u32[]{:S(2)}, u32[]{:S(2)}) collective-permute-start(bf16[4,4,1,8,640]{4,3,2,1,0:T(8,128)(2,1)S(1)} %get-tuple-element.48), channel_id=1, source_target_pairs={{0,64},{64,128},{128,192},{192,0},{256,320},{320,384},{384,448},{4... | collective-permute-start | bytes 491528 | tf_op jit(solution)/shard_map/ppermute | solution.py:80
  75.7 11.9 %collective-permute-start.4 = (bf16[4,4,1,8,640]{4,3,2,1,0:T(8,128)(2,1)S(1)}, bf16[4,4,1,8,640]{4,3,2,1,0:T(8,128)(2,1)S(1)}, u32[]{:S(2)}, u32[]{:S(2)}) collective-permute-start(bf16[4,4,1,8,640]{4,3,2,1,0:T(8,128)(2,1)S(1)} %get-tuple-element.47), channel_id=1, source_target_pairs={{0,128},{64,192},{128,0},{192,64},{256,384},{320,448},{384,256},{4... | collective-permute-start | bytes 491528 | tf_op jit(solution)/shard_map/ppermute | solution.py:80
  87.5 3.6 %collective-permute-start.5 = (bf16[4,4,1,8,640]{4,3,2,1,0:T(8,128)(2,1)S(1)}, bf16[4,4,1,8,640]{4,3,2,1,0:T(8,128)(2,1)S(1)}, u32[]{:S(2)}, u32[]{:S(2)}) collective-permute-start(bf16[4,4,1,8,640]{4,3,2,1,0:T(8,128)(2,1)S(1)} %get-tuple-element.46), channel_id=1, source_target_pairs={{0,192},{64,0},{128,64},{192,128},{256,448},{320,256},{384,320},{4... | collective-permute-start | bytes 491528 | tf_op jit(solution)/shard_map/ppermute | solution.py:80
  91.9 6.1 %collective-permute-start.6 = (bf16[4,4,1,8,640]{4,3,2,1,0:T(8,128)(2,1)S(1)}, bf16[4,4,1,8,640]{4,3,2,1,0:T(8,128)(2,1)S(1)}, u32[]{:S(2)}, u32[]{:S(2)}) collective-permute-start(bf16[4,4,1,8,640]{4,3,2,1,0:T(8,128)(2,1)S(1)} %get-tuple-element.44), channel_id=1, source_target_pairs={{0,64},{64,128},{128,192},{192,0},{256,320},{320,384},{384,448},{4... | collective-permute-start | bytes 491528 | tf_op jit(solution)/shard_map/ppermute | solution.py:80
  98.0 3.1 %collective-permute-start.7 = (bf16[4,4,1,8,640]{4,3,2,1,0:T(8,128)(2,1)S(1)}, bf16[4,4,1,8,640]{4,3,2,1,0:T(8,128)(2,1)S(1)}, u32[]{:S(2)}, u32[]{:S(2)}) collective-permute-start(bf16[4,4,1,8,640]{4,3,2,1,0:T(8,128)(2,1)S(1)} %get-tuple-element.43), channel_id=1, source_target_pairs={{0,128},{64,192},{128,0},{192,64},{256,384},{320,448},{384,256},{4... | collective-permute-start | bytes 491528 | tf_op jit(solution)/shard_map/ppermute | solution.py:80
  101.2 6.1 %collective-permute-start.8 = (bf16[4,4,1,8,640]{4,3,2,1,0:T(8,128)(2,1)S(1)}, bf16[4,4,1,8,640]{4,3,2,1,0:T(8,128)(2,1)S(1)}, u32[]{:S(2)}, u32[]{:S(2)}) collective-permute-start(bf16[4,4,1,8,640]{4,3,2,1,0:T(8,128)(2,1)S(1)} %get-tuple-element.42), channel_id=1, source_target_pairs={{0,192},{64,0},{128,64},{192,128},{256,448},{320,256},{384,320},{4... | collective-permute-start | bytes 491528 | tf_op jit(solution)/shard_map/ppermute | solution.py:80
  109.3 46.2 %collective-permute-done.5.refs_3_ = bf16[4,4,1,8,640]{4,3,2,1,0:T(8,128)(2,1)S(1)} collective-permute-done((bf16[4,4,1,8,640]{4,3,2,1,0:T(8,128)(2,1)S(1)}, bf16[4,4,1,8,640]{4,3,2,1,0:T(8,128)(2,1)S(1)}, u32[]{:S(2)}, u32[]{:S(2)}) %collective-permute-start.5) | collective-permute-done | bytes 163872 | tf_op jit(solution)/shard_map/ppermute | solution.py:80
  156.2 4.9 %shard_map.76 = (bf16[4,4,1,8,640]{4,3,2,1,0:T(8,128)(2,1)}, bf16[4,4,1,8,640]{4,3,2,1,0:T(8,128)(2,1)}, bf16[4,4,1,8,640]{4,3,2,1,0:T(8,128)(2,1)}, bf16[4,4,1,8,640]{4,3,2,1,0:T(8,128)(2,1)}) custom-call(bf16[4,4,1,8,640]{4,3,2,1,0:T(8,128)(2,1)} %get-tuple-element.49.refs_0_, bf16[4,4,1,8,640]{4,3,2,1,0:T(8,128)(2,1)} %copy-done.7, ...), custom_call_target="tpu_custom_call" | custom-call | tf_op jit(solution)/shard_map/pallas_call | solution.py:63
  161.1 17.6 %collective-permute-start.9 = (bf16[4,4,1,8,640]{4,3,2,1,0:T(8,128)(2,1)}, bf16[4,4,1,8,640]{4,3,2,1,0:T(8,128)(2,1)S(1)}, u32[]{:S(2)}, u32[]{:S(2)}) collective-permute-start(bf16[4,4,1,8,640]{4,3,2,1,0:T(8,128)(2,1)} %get-tuple-element.14), channel_id=1, source_target_pairs={{0,192},{64,0},{128,64},{192,128},{256,448},{320,256},{384,320},{4... | collective-permute-start | bytes 491528 | tf_op jit(solution)/shard_map/ppermute | solution.py:80
  178.7 25.3 %collective-permute-start.11 = (bf16[4,4,1,8,640]{4,3,2,1,0:T(8,128)(2,1)}, bf16[4,4,1,8,640]{4,3,2,1,0:T(8,128)(2,1)S(1)}, u32[]{:S(2)}, u32[]{:S(2)}) collective-permute-start(bf16[4,4,1,8,640]{4,3,2,1,0:T(8,128)(2,1)} %get-tuple-element.16), channel_id=1, source_target_pairs={{0,128},{64,192},{128,0},{192,64},{256,384},{320,448},{384,256},{4... | collective-permute-start | bytes 491528 | tf_op jit(solution)/shard_map/ppermute | solution.py:80
  204.8 4.8 %shard_map.77 = (bf16[4,4,1,8,640]{4,3,2,1,0:T(8,128)(2,1)}, bf16[4,4,1,8,640]{4,3,2,1,0:T(8,128)(2,1)}, bf16[4,4,1,8,640]{4,3,2,1,0:T(8,128)(2,1)}, bf16[4,4,1,8,640]{4,3,2,1,0:T(8,128)(2,1)}) custom-call(bf16[4,4,1,8,640]{4,3,2,1,0:T(8,128)(2,1)} %get-tuple-element.45.refs_0_, bf16[4,4,1,8,640]{4,3,2,1,0:T(8,128)(2,1)} %copy-done.5, ...), custom_call_target="tpu_custom_call" | custom-call | tf_op jit(solution)/shard_map/pallas_call | solution.py:63
  214.1 12.6 %collective-permute-start.12 = (bf16[4,4,1,8,640]{4,3,2,1,0:T(8,128)(2,1)S(1)}, bf16[4,4,1,8,640]{4,3,2,1,0:T(8,128)(2,1)S(1)}, u32[]{:S(2)}, u32[]{:S(2)}) collective-permute-start(bf16[4,4,1,8,640]{4,3,2,1,0:T(8,128)(2,1)S(1)} %copy-done.13), channel_id=1, source_target_pairs={{0,128},{64,192},{128,0},{192,64},{256,384},{320,448},{384,256},{4... | collective-permute-start | bytes 491528 | tf_op jit(solution)/shard_map/ppermute | solution.py:80
  231.3 8.6 %collective-permute-done.13 = bf16[4,4,1,8,640]{4,3,2,1,0:T(8,128)(2,1)S(1)} collective-permute-done((bf16[4,4,1,8,640]{4,3,2,1,0:T(8,128)(2,1)S(1)}, bf16[4,4,1,8,640]{4,3,2,1,0:T(8,128)(2,1)S(1)}, u32[]{:S(2)}, u32[]{:S(2)}) %collective-permute-start.13) | collective-permute-done | bytes 163872 | tf_op jit(solution)/shard_map/ppermute | solution.py:80
  240.2 10.0 %collective-permute-start.15 = (bf16[4,4,2,8,640]{4,3,2,1,0:T(8,128)(2,1)S(1)}, bf16[4,4,2,8,640]{4,3,2,1,0:T(8,128)(2,1)S(1)}, u32[]{:S(2)}, u32[]{:S(2)}) collective-permute-start(bf16[4,4,2,8,640]{4,3,2,1,0:T(8,128)(2,1)S(1)} %pad_maximum_fusion.3), channel_id=1, source_target_pairs={{0,768},{64,832},{128,896},{192,960},{256,0},{320,64},{384,128},{4... | collective-permute-start | bytes 983048 | tf_op jit(solution)/shard_map/ppermute | solution.py:80
  252.2 4.2 %collective-permute-start.16 = (bf16[4,4,2,8,640]{4,3,2,1,0:T(8,128)(2,1)S(1)}, bf16[4,4,2,8,640]{4,3,2,1,0:T(8,128)(2,1)S(1)}, u32[]{:S(2)}, u32[]{:S(2)}) collective-permute-start(bf16[4,4,2,8,640]{4,3,2,1,0:T(8,128)(2,1)S(1)} %pad_maximum_fusion.4), channel_id=1, source_target_pairs={{0,512},{64,576},{128,640},{192,704},{256,768},{320,832},{384,896}... | collective-permute-start | bytes 983048 | tf_op jit(solution)/shard_map/ppermute | solution.py:80
  258.3 5.6 %collective-permute-done.16 = bf16[4,4,2,8,640]{4,3,2,1,0:T(8,128)(2,1)S(1)} collective-permute-done((bf16[4,4,2,8,640]{4,3,2,1,0:T(8,128)(2,1)S(1)}, bf16[4,4,2,8,640]{4,3,2,1,0:T(8,128)(2,1)S(1)}, u32[]{:S(2)}, u32[]{:S(2)}) %collective-permute-start.16) | collective-permute-done | bytes 327712 | tf_op jit(solution)/shard_map/ppermute | solution.py:80
  (103 shorter events, 32.4 us)
Async XLA Ops:
  4.0 49.7 %all-to-all-start = ((bf16[64,4,1,4,640]{4,3,2,1,0:T(4,128)(2,1)}), bf16[64,4,1,4,640]{4,3,2,1,0:T(4,128)(2,1)S(1)}, u32[]{:S(2)}, u32[]{:S(2)}) async-start(bf16[64,4,1,4,640]{4,3,2,1,0:T(4,128)(2,1)} %pad_maximum_fusion), calls=%async_computation | async-start | bytes 2621440 | tf_op jit(solution)/shard_map/all_to_all | solution.py:93
  21.1 19.9 %collective-permute-start = (bf16[4,4,2,8,640]{4,3,2,1,0:T(8,128)(2,1)S(1)}, bf16[4,4,2,8,640]{4,3,2,1,0:T(8,128)(2,1)S(1)}, u32[]{:S(2)}, u32[]{:S(2)}) collective-permute-start(bf16[4,4,2,8,640]{4,3,2,1,0:T(8,128)(2,1)S(1)} %bitcast.122), channel_id=1, source_target_pairs={{0,256},{64,320},{128,384},{192,448},{256,512},{320,576},{384,640}... | collective-permute-start | bytes 983048 | tf_op jit(solution)/shard_map/ppermute | solution.py:80
  23.1 17.9 %collective-permute-start.1 = (bf16[4,4,2,8,640]{4,3,2,1,0:T(8,128)(2,1)S(1)}, bf16[4,4,2,8,640]{4,3,2,1,0:T(8,128)(2,1)}, u32[]{:S(2)}, u32[]{:S(2)}) collective-permute-start(bf16[4,4,2,8,640]{4,3,2,1,0:T(8,128)(2,1)S(1)} %bitcast.123), channel_id=1, source_target_pairs={{0,512},{64,576},{128,640},{192,704},{256,768},{320,832},{384,896}... | collective-permute-start | bytes 983048 | tf_op jit(solution)/shard_map/ppermute | solution.py:80
  25.6 18.1 %collective-permute-start.2 = (bf16[4,4,2,8,640]{4,3,2,1,0:T(8,128)(2,1)S(1)}, bf16[4,4,2,8,640]{4,3,2,1,0:T(8,128)(2,1)}, u32[]{:S(2)}, u32[]{:S(2)}) collective-permute-start(bf16[4,4,2,8,640]{4,3,2,1,0:T(8,128)(2,1)S(1)} %bitcast.124), channel_id=1, source_target_pairs={{0,768},{64,832},{128,896},{192,960},{256,0},{320,64},{384,128},{4... | collective-permute-start | bytes 983048 | tf_op jit(solution)/shard_map/ppermute | solution.py:80
  61.3 204.5 %all-to-all-start.1 = ((bf16[64,4,1,4,640]{4,3,2,1,0:T(4,128)(2,1)}), bf16[64,4,1,4,640]{4,3,2,1,0:T(4,128)(2,1)S(1)}, u32[]{:S(2)}, u32[]{:S(2)}) async-start(bf16[64,4,1,4,640]{4,3,2,1,0:T(4,128)(2,1)} %shard_map.75), calls=%async_computation.1 | async-start | bytes 2621440 | tf_op jit(solution)/shard_map/all_to_all | solution.py:93
  68.5 32.6 %collective-permute-start.3 = (bf16[4,4,1,8,640]{4,3,2,1,0:T(8,128)(2,1)S(1)}, bf16[4,4,1,8,640]{4,3,2,1,0:T(8,128)(2,1)S(1)}, u32[]{:S(2)}, u32[]{:S(2)}) collective-permute-start(bf16[4,4,1,8,640]{4,3,2,1,0:T(8,128)(2,1)S(1)} %get-tuple-element.48), channel_id=1, source_target_pairs={{0,64},{64,128},{128,192},{192,0},{256,320},{320,384},{384,448},{4... | collective-permute-start | bytes 491528 | tf_op jit(solution)/shard_map/ppermute | solution.py:80
  75.7 33.7 %collective-permute-start.4 = (bf16[4,4,1,8,640]{4,3,2,1,0:T(8,128)(2,1)S(1)}, bf16[4,4,1,8,640]{4,3,2,1,0:T(8,128)(2,1)S(1)}, u32[]{:S(2)}, u32[]{:S(2)}) collective-permute-start(bf16[4,4,1,8,640]{4,3,2,1,0:T(8,128)(2,1)S(1)} %get-tuple-element.47), channel_id=1, source_target_pairs={{0,128},{64,192},{128,0},{192,64},{256,384},{320,448},{384,256},{4... | collective-permute-start | bytes 491528 | tf_op jit(solution)/shard_map/ppermute | solution.py:80
  87.5 68.0 %collective-permute-start.5 = (bf16[4,4,1,8,640]{4,3,2,1,0:T(8,128)(2,1)S(1)}, bf16[4,4,1,8,640]{4,3,2,1,0:T(8,128)(2,1)S(1)}, u32[]{:S(2)}, u32[]{:S(2)}) collective-permute-start(bf16[4,4,1,8,640]{4,3,2,1,0:T(8,128)(2,1)S(1)} %get-tuple-element.46), channel_id=1, source_target_pairs={{0,192},{64,0},{128,64},{192,128},{256,448},{320,256},{384,320},{4... | collective-permute-start | bytes 491528 | tf_op jit(solution)/shard_map/ppermute | solution.py:80
  91.9 112.1 %collective-permute-start.6 = (bf16[4,4,1,8,640]{4,3,2,1,0:T(8,128)(2,1)S(1)}, bf16[4,4,1,8,640]{4,3,2,1,0:T(8,128)(2,1)S(1)}, u32[]{:S(2)}, u32[]{:S(2)}) collective-permute-start(bf16[4,4,1,8,640]{4,3,2,1,0:T(8,128)(2,1)S(1)} %get-tuple-element.44), channel_id=1, source_target_pairs={{0,64},{64,128},{128,192},{192,0},{256,320},{320,384},{384,448},{4... | collective-permute-start | bytes 491528 | tf_op jit(solution)/shard_map/ppermute | solution.py:80
  98.0 106.0 %collective-permute-start.7 = (bf16[4,4,1,8,640]{4,3,2,1,0:T(8,128)(2,1)S(1)}, bf16[4,4,1,8,640]{4,3,2,1,0:T(8,128)(2,1)S(1)}, u32[]{:S(2)}, u32[]{:S(2)}) collective-permute-start(bf16[4,4,1,8,640]{4,3,2,1,0:T(8,128)(2,1)S(1)} %get-tuple-element.43), channel_id=1, source_target_pairs={{0,128},{64,192},{128,0},{192,64},{256,384},{320,448},{384,256},{4... | collective-permute-start | bytes 491528 | tf_op jit(solution)/shard_map/ppermute | solution.py:80
  101.1 54.4 %copy-start.7 = (bf16[4,4,1,8,640]{4,3,2,1,0:T(8,128)(2,1)}, bf16[4,4,1,8,640]{4,3,2,1,0:T(8,128)(2,1)S(1)}, u32[]{:S(2)}) copy-start(bf16[4,4,1,8,640]{4,3,2,1,0:T(8,128)(2,1)S(1)} %collective-permute-done.3.refs_1_) | copy-start | bytes 491524
  101.2 102.9 %collective-permute-start.8 = (bf16[4,4,1,8,640]{4,3,2,1,0:T(8,128)(2,1)S(1)}, bf16[4,4,1,8,640]{4,3,2,1,0:T(8,128)(2,1)S(1)}, u32[]{:S(2)}, u32[]{:S(2)}) collective-permute-start(bf16[4,4,1,8,640]{4,3,2,1,0:T(8,128)(2,1)S(1)} %get-tuple-element.42), channel_id=1, source_target_pairs={{0,192},{64,0},{128,64},{192,128},{256,448},{320,256},{384,320},{4... | collective-permute-start | bytes 491528 | tf_op jit(solution)/shard_map/ppermute | solution.py:80
  109.3 46.2 %copy-start.8 = (bf16[4,4,1,8,640]{4,3,2,1,0:T(8,128)(2,1)}, bf16[4,4,1,8,640]{4,3,2,1,0:T(8,128)(2,1)S(1)}, u32[]{:S(2)}) copy-start(bf16[4,4,1,8,640]{4,3,2,1,0:T(8,128)(2,1)S(1)} %collective-permute-done.4.refs_2_) | copy-start | bytes 491524
  161.1 67.6 %copy-start.11 = (bf16[4,4,1,8,640]{4,3,2,1,0:T(8,128)(2,1)S(1)}, bf16[4,4,1,8,640]{4,3,2,1,0:T(8,128)(2,1)}, u32[]{:S(2)}) copy-start(bf16[4,4,1,8,640]{4,3,2,1,0:T(8,128)(2,1)} %get-tuple-element.18) | copy-start | bytes 491524
  161.1 67.6 %collective-permute-start.9 = (bf16[4,4,1,8,640]{4,3,2,1,0:T(8,128)(2,1)}, bf16[4,4,1,8,640]{4,3,2,1,0:T(8,128)(2,1)S(1)}, u32[]{:S(2)}, u32[]{:S(2)}) collective-permute-start(bf16[4,4,1,8,640]{4,3,2,1,0:T(8,128)(2,1)} %get-tuple-element.14), channel_id=1, source_target_pairs={{0,192},{64,0},{128,64},{192,128},{256,448},{320,256},{384,320},{4... | collective-permute-start | bytes 491528 | tf_op jit(solution)/shard_map/ppermute | solution.py:80
  178.7 52.5 %collective-permute-start.11 = (bf16[4,4,1,8,640]{4,3,2,1,0:T(8,128)(2,1)}, bf16[4,4,1,8,640]{4,3,2,1,0:T(8,128)(2,1)S(1)}, u32[]{:S(2)}, u32[]{:S(2)}) collective-permute-start(bf16[4,4,1,8,640]{4,3,2,1,0:T(8,128)(2,1)} %get-tuple-element.16), channel_id=1, source_target_pairs={{0,128},{64,192},{128,0},{192,64},{256,384},{320,448},{384,256},{4... | collective-permute-start | bytes 491528 | tf_op jit(solution)/shard_map/ppermute | solution.py:80
  209.6 17.1 %copy-start.12 = (bf16[4,4,1,8,640]{4,3,2,1,0:T(8,128)(2,1)S(1)}, bf16[4,4,1,8,640]{4,3,2,1,0:T(8,128)(2,1)}, u32[]{:S(2)}) copy-start(bf16[4,4,1,8,640]{4,3,2,1,0:T(8,128)(2,1)} %get-tuple-element.19) | copy-start | bytes 491524
  211.6 28.2 %collective-permute-start.10 = (bf16[4,4,1,8,640]{4,3,2,1,0:T(8,128)(2,1)S(1)}, bf16[4,4,1,8,640]{4,3,2,1,0:T(8,128)(2,1)S(1)}, u32[]{:S(2)}, u32[]{:S(2)}) collective-permute-start(bf16[4,4,1,8,640]{4,3,2,1,0:T(8,128)(2,1)S(1)} %copy-done.14), channel_id=1, source_target_pairs={{0,192},{64,0},{128,64},{192,128},{256,448},{320,256},{384,320},{4... | collective-permute-start | bytes 491528 | tf_op jit(solution)/shard_map/ppermute | solution.py:80
  214.1 25.8 %collective-permute-start.12 = (bf16[4,4,1,8,640]{4,3,2,1,0:T(8,128)(2,1)S(1)}, bf16[4,4,1,8,640]{4,3,2,1,0:T(8,128)(2,1)S(1)}, u32[]{:S(2)}, u32[]{:S(2)}) collective-permute-start(bf16[4,4,1,8,640]{4,3,2,1,0:T(8,128)(2,1)S(1)} %copy-done.13), channel_id=1, source_target_pairs={{0,128},{64,192},{128,0},{192,64},{256,384},{320,448},{384,256},{4... | collective-permute-start | bytes 491528 | tf_op jit(solution)/shard_map/ppermute | solution.py:80
  226.8 13.2 %collective-permute-start.14 = (bf16[4,4,1,8,640]{4,3,2,1,0:T(8,128)(2,1)S(1)}, bf16[4,4,1,8,640]{4,3,2,1,0:T(8,128)(2,1)S(1)}, u32[]{:S(2)}, u32[]{:S(2)}) collective-permute-start(bf16[4,4,1,8,640]{4,3,2,1,0:T(8,128)(2,1)S(1)} %copy-done.12), channel_id=1, source_target_pairs={{0,64},{64,128},{128,192},{192,0},{256,320},{320,384},{384,448},{4... | collective-permute-start | bytes 491528 | tf_op jit(solution)/shard_map/ppermute | solution.py:80
  228.7 11.1 %collective-permute-start.13 = (bf16[4,4,1,8,640]{4,3,2,1,0:T(8,128)(2,1)S(1)}, bf16[4,4,1,8,640]{4,3,2,1,0:T(8,128)(2,1)S(1)}, u32[]{:S(2)}, u32[]{:S(2)}) collective-permute-start(bf16[4,4,1,8,640]{4,3,2,1,0:T(8,128)(2,1)S(1)} %copy-done.11), channel_id=1, source_target_pairs={{0,64},{64,128},{128,192},{192,0},{256,320},{320,384},{384,448},{4... | collective-permute-start | bytes 491528 | tf_op jit(solution)/shard_map/ppermute | solution.py:80
  240.2 18.1 %collective-permute-start.15 = (bf16[4,4,2,8,640]{4,3,2,1,0:T(8,128)(2,1)S(1)}, bf16[4,4,2,8,640]{4,3,2,1,0:T(8,128)(2,1)S(1)}, u32[]{:S(2)}, u32[]{:S(2)}) collective-permute-start(bf16[4,4,2,8,640]{4,3,2,1,0:T(8,128)(2,1)S(1)} %pad_maximum_fusion.3), channel_id=1, source_target_pairs={{0,768},{64,832},{128,896},{192,960},{256,0},{320,64},{384,128},{4... | collective-permute-start | bytes 983048 | tf_op jit(solution)/shard_map/ppermute | solution.py:80
  250.2 14.5 %collective-permute-start.17 = (bf16[4,4,2,8,640]{4,3,2,1,0:T(8,128)(2,1)S(1)}, bf16[4,4,2,8,640]{4,3,2,1,0:T(8,128)(2,1)S(1)}, u32[]{:S(2)}, u32[]{:S(2)}) collective-permute-start(bf16[4,4,2,8,640]{4,3,2,1,0:T(8,128)(2,1)S(1)} %pad_maximum_fusion.5), channel_id=1, source_target_pairs={{0,256},{64,320},{128,384},{192,448},{256,512},{320,576},{384,640}... | collective-permute-start | bytes 983048 | tf_op jit(solution)/shard_map/ppermute | solution.py:80
  252.2 11.7 %collective-permute-start.16 = (bf16[4,4,2,8,640]{4,3,2,1,0:T(8,128)(2,1)S(1)}, bf16[4,4,2,8,640]{4,3,2,1,0:T(8,128)(2,1)S(1)}, u32[]{:S(2)}, u32[]{:S(2)}) collective-permute-start(bf16[4,4,2,8,640]{4,3,2,1,0:T(8,128)(2,1)S(1)} %pad_maximum_fusion.4), channel_id=1, source_target_pairs={{0,512},{64,576},{128,640},{192,704},{256,768},{320,832},{384,896}... | collective-permute-start | bytes 983048 | tf_op jit(solution)/shard_map/ppermute | solution.py:80
  (11 other events, 43.9 us)

commit v3 on v2

--- a/solution.py
+++ b/solution.py
@@ -9,7 +9,6 @@
 HEAD_DIM = 64
 HEAD_PAIR = 2 * HEAD_DIM
 FACTOR = 4
-CHUNKS = 2
 
 
 def attend(x_refs, o_refs, item, lanes):
@@ -45,8 +44,9 @@
     totals = (totals[0], totals[1] * scale, totals[2] * scale, totals[3])
     for t in range(tensors):
         done = totals[t].astype(jnp.bfloat16) if full_tiles else totals[t]
+        done = done.reshape(len(x_refs), sources, rows, HEAD_PAIR)
         for i, r in enumerate(o_refs):
-            piece = done[i * part : (i + 1) * part].reshape(sources, rows, HEAD_PAIR)
+            piece = done[:, i] if len(o_refs) > 1 else done[0]
             r[:, t, item, :, lanes] = piece.astype(jnp.bfloat16)
 
 
@@ -87,7 +87,6 @@
     lat = lax.axis_size("lat")
     lon_items = batch * rows // lon
     lat_items = batch * cols // lat
-    part = lat_items // CHUNKS
     me = lax.axis_index("lat")
     near, far = me // FACTOR, me % FACTOR
     swap_lon = lambda t: lax.all_to_all(t, "lon", split_axis=0, concat_axis=0, tiled=True)
@@ -97,17 +96,14 @@
     send = jnp.stack([t.transpose(0, 2, 1, 3).reshape(lat, lat_items, rows, feats) for t in inputs], axis=1)
     send = send.reshape((FACTOR, FACTOR) + send.shape[1:])
     turned = jnp.stack([shift(pick(send, near + m), False, m) for m in range(FACTOR)], axis=1)
-    home = []
-    for c in range(CHUNKS):
-        mine = turned[:, :, :, c * part : (c + 1) * part]
-        got = [shift(pick(mine, far + k), True, k) for k in range(FACTOR)]
-        done = attention(got)
-        home.append([shift(done[k], True, -k) for k in range(FACTOR)])
+    lat_got = [shift(pick(turned, far + k), True, k) for k in range(FACTOR)]
     (lon_done,) = attention([lon_got])
     lon_back = swap_lon(lon_done)
-    joined = [jnp.concatenate([h[k] for h in home], axis=2) for k in range(FACTOR)]
-    back = [shift(jnp.stack([j[m] for j in joined], axis=0), False, -m) for m in range(FACTOR)]
-    lat_back = jnp.roll(jnp.roll(jnp.stack(back, axis=0), near, axis=0), far, axis=1)
+    lat_done = attention(lat_got)
+    back = [shift(lat_done[m], False, -m) for m in range(FACTOR)]
+    home = [shift(jnp.stack([b[k] for b in back], axis=0), True, -k) for k in range(FACTOR)]
+    lat_back = jnp.stack([pick(jnp.stack(home, axis=0), z - far) for z in range(FACTOR)], axis=1)
+    lat_back = jnp.stack([pick(lat_back, x - near) for x in range(FACTOR)], axis=0)
     lat_back = lat_back.reshape((lat,) + lat_back.shape[2:])
     results = []
     for i in range(tensors):

time: 271 us -> 264 us (0.974)
  the two profiles are of different devices: /device:TPU:128 before, /device:TPU:205 now
where the time goes in v3:
time: 264 us
  waiting for transfers between devices  116 us (44%)
  starting transfers between devices  74.3 us (28%)
  blocking collectives  43.4 us (16%)
  Pallas kernels  14.4 us (5%)
  local copies, waits for them, and re-layouts  9.66 us (4%)
  other arithmetic  4.68 us (2%)
    ppermute x12, waiting for transfers between devices, shift(): return lax.ppermute(piece, 'lat', pairs)  116 us
    ppermute x12, starting transfers between devices, shift(): return lax.ppermute(piece, 'lat', pairs)  66.3 us
    all_to_all x1, blocking collectives, on_device(): lax.all_to_all(t, 'lon', split_axis=0, concat_axis=0, tiled=True)  43.4 us
    pallas_call x2, Pallas kernels, attention(): pl.pallas_call(attention_kernel, in_specs=[spec] * len(pieces), out_specs...  14.4 us
    all_to_all x1, starting transfers between devices, on_device(): lax.all_to_all(t, 'lon', split_axis=0, concat_axis=0, tiled=True)  7.95 us
  transfers between devices with their start and end apart: 13, of which 10 were waited for; matrix products, arithmetic and copies ran while one was open for 2% of the time, Pallas kernels for 3%

profile of v3, /device:TPU:205, one launch (start us, length us, event | category | flops | bytes accessed | tf_op | source)
XLA Modules:
  0.0 263.6 jit_solution(2423366375094718771)
XLA Ops:
  2.9 43.4 %all_to_all.10.refs_0_ = bf16[64,4,1,4,640]{4,3,2,1,0:T(4,128)(2,1)} all-to-all(bf16[64,4,1,4,640]{4,3,2,1,0:T(4,128)(2,1)S(1)} %pad_maximum_fusion), channel_id=1, replica_groups=mesh['lat'=16,'lon'=64] {'lon'}, dimensions={0} | all-to-all | bytes 2621440 | tf_op jit(solution)/shard_map/all_to_all | solution.py:92
  46.3 6.5 %shard_map.75 = bf16[64,4,1,4,640]{4,3,2,1,0:T(4,128)(2,1)} custom-call(bf16[64,4,1,4,640]{4,3,2,1,0:T(4,128)(2,1)} %all_to_all.10.refs_0_), custom_call_target="tpu_custom_call" | custom-call | tf_op jit(solution)/shard_map/pallas_call | solution.py:63
  52.8 7.9 %all-to-all-start.1 = ((bf16[64,4,1,4,640]{4,3,2,1,0:T(4,128)(2,1)}), bf16[64,4,1,4,640]{4,3,2,1,0:T(4,128)(2,1)S(1)}, u32[]{:S(2)}, u32[]{:S(2)}) async-start(bf16[64,4,1,4,640]{4,3,2,1,0:T(4,128)(2,1)} %shard_map.75), calls=%async_computation.1 | async-start | bytes 2621440 | tf_op jit(solution)/shard_map/all_to_all | solution.py:92
  62.3 2.8 %collective-permute-start = (bf16[4,4,2,8,640]{4,3,2,1,0:T(8,128)(2,1)S(1)}, bf16[4,4,2,8,640]{4,3,2,1,0:T(8,128)(2,1)S(1)}, u32[]{:S(2)}, u32[]{:S(2)}) collective-permute-start(bf16[4,4,2,8,640]{4,3,2,1,0:T(8,128)(2,1)S(1)} %bitcast.117), channel_id=1, source_target_pairs={{0,256},{64,320},{128,384},{192,448},{256,512},{320,576},{384,640}... | collective-permute-start | bytes 983048 | tf_op jit(solution)/shard_map/ppermute | solution.py:80
  65.9 4.9 %collective-permute-start.1 = (bf16[4,4,2,8,640]{4,3,2,1,0:T(8,128)(2,1)}, bf16[4,4,2,8,640]{4,3,2,1,0:T(8,128)(2,1)S(1)}, u32[]{:S(2)}, u32[]{:S(2)}) collective-permute-start(bf16[4,4,2,8,640]{4,3,2,1,0:T(8,128)(2,1)} %bitcast.90), channel_id=1, source_target_pairs={{0,512},{64,576},{128,640},{192,704},{256,768},{320,832},{384,896}... | collective-permute-start | bytes 983048 | tf_op jit(solution)/shard_map/ppermute | solution.py:80
  71.6 4.0 %collective-permute-start.2 = (bf16[4,4,2,8,640]{4,3,2,1,0:T(8,128)(2,1)}, bf16[4,4,2,8,640]{4,3,2,1,0:T(8,128)(2,1)S(1)}, u32[]{:S(2)}, u32[]{:S(2)}) collective-permute-start(bf16[4,4,2,8,640]{4,3,2,1,0:T(8,128)(2,1)} %bitcast.89), channel_id=1, source_target_pairs={{0,768},{64,832},{128,896},{192,960},{256,0},{320,64},{384,128},{4... | collective-permute-start | bytes 983048 | tf_op jit(solution)/shard_map/ppermute | solution.py:80
  75.7 7.2 %collective-permute-done.1 = bf16[4,4,2,8,640]{4,3,2,1,0:T(8,128)(2,1)S(1)} collective-permute-done((bf16[4,4,2,8,640]{4,3,2,1,0:T(8,128)(2,1)}, bf16[4,4,2,8,640]{4,3,2,1,0:T(8,128)(2,1)S(1)}, u32[]{:S(2)}, u32[]{:S(2)}) %collective-permute-start.1) | collective-permute-done | bytes 327712 | tf_op jit(solution)/shard_map/ppermute | solution.py:80
  82.8 3.5 %collective-permute-done.2 = bf16[4,4,2,8,640]{4,3,2,1,0:T(8,128)(2,1)S(1)} collective-permute-done((bf16[4,4,2,8,640]{4,3,2,1,0:T(8,128)(2,1)}, bf16[4,4,2,8,640]{4,3,2,1,0:T(8,128)(2,1)S(1)}, u32[]{:S(2)}, u32[]{:S(2)}) %collective-permute-start.2) | collective-permute-done | bytes 327712 | tf_op jit(solution)/shard_map/ppermute | solution.py:80
  87.4 13.5 %collective-permute-start.5 = (bf16[4,4,2,8,640]{4,3,2,1,0:T(8,128)(2,1)S(1)}, bf16[4,4,2,8,640]{4,3,2,1,0:T(8,128)(2,1)S(1)}, u32[]{:S(2)}, u32[]{:S(2)}) collective-permute-start(bf16[4,4,2,8,640]{4,3,2,1,0:T(8,128)(2,1)S(1)} %get-tuple-element.36), channel_id=1, source_target_pairs={{0,192},{64,0},{128,64},{192,128},{256,448},{320,256},{384,320},{4... | collective-permute-start | bytes 983048 | tf_op jit(solution)/shard_map/ppermute | solution.py:80
  100.9 3.1 %collective-permute-start.4 = (bf16[4,4,2,8,640]{4,3,2,1,0:T(8,128)(2,1)S(1)}, bf16[4,4,2,8,640]{4,3,2,1,0:T(8,128)(2,1)S(1)}, u32[]{:S(2)}, u32[]{:S(2)}) collective-permute-start(bf16[4,4,2,8,640]{4,3,2,1,0:T(8,128)(2,1)S(1)} %get-tuple-element.37), channel_id=1, source_target_pairs={{0,128},{64,192},{128,0},{192,64},{256,384},{320,448},{384,256},{4... | collective-permute-start | bytes 983048 | tf_op jit(solution)/shard_map/ppermute | solution.py:80
  104.0 7.5 %collective-permute-start.3 = (bf16[4,4,2,8,640]{4,3,2,1,0:T(8,128)(2,1)S(1)}, bf16[4,4,2,8,640]{4,3,2,1,0:T(8,128)(2,1)S(1)}, u32[]{:S(2)}, u32[]{:S(2)}) collective-permute-start(bf16[4,4,2,8,640]{4,3,2,1,0:T(8,128)(2,1)S(1)} %get-tuple-element.38), channel_id=1, source_target_pairs={{0,64},{64,128},{128,192},{192,0},{256,320},{320,384},{384,448},{4... | collective-permute-start | bytes 983048 | tf_op jit(solution)/shard_map/ppermute | solution.py:80
  111.4 6.3 %collective-permute-done.5.refs_3_ = bf16[4,4,2,8,640]{4,3,2,1,0:T(8,128)(2,1)S(1)} collective-permute-done((bf16[4,4,2,8,640]{4,3,2,1,0:T(8,128)(2,1)S(1)}, bf16[4,4,2,8,640]{4,3,2,1,0:T(8,128)(2,1)S(1)}, u32[]{:S(2)}, u32[]{:S(2)}) %collective-permute-start.5) | collective-permute-done | bytes 327712 | tf_op jit(solution)/shard_map/ppermute | solution.py:80
  117.7 33.8 %collective-permute-done.4.refs_2_ = bf16[4,4,2,8,640]{4,3,2,1,0:T(8,128)(2,1)S(1)} collective-permute-done((bf16[4,4,2,8,640]{4,3,2,1,0:T(8,128)(2,1)S(1)}, bf16[4,4,2,8,640]{4,3,2,1,0:T(8,128)(2,1)S(1)}, u32[]{:S(2)}, u32[]{:S(2)}) %collective-permute-start.4) | collective-permute-done | bytes 327712 | tf_op jit(solution)/shard_map/ppermute | solution.py:80
  151.5 10.1 %collective-permute-done.3.refs_1_ = bf16[4,4,2,8,640]{4,3,2,1,0:T(8,128)(2,1)S(1)} collective-permute-done((bf16[4,4,2,8,640]{4,3,2,1,0:T(8,128)(2,1)S(1)}, bf16[4,4,2,8,640]{4,3,2,1,0:T(8,128)(2,1)S(1)}, u32[]{:S(2)}, u32[]{:S(2)}) %collective-permute-start.3) | collective-permute-done | bytes 327712 | tf_op jit(solution)/shard_map/ppermute | solution.py:80
  162.3 7.9 %shard_map.76 = (bf16[4,4,2,8,640]{4,3,2,1,0:T(8,128)(2,1)}, bf16[4,4,2,8,640]{4,3,2,1,0:T(8,128)(2,1)}, bf16[4,4,2,8,640]{4,3,2,1,0:T(8,128)(2,1)}, bf16[4,4,2,8,640]{4,3,2,1,0:T(8,128)(2,1)}) custom-call(bf16[4,4,2,8,640]{4,3,2,1,0:T(8,128)(2,1)} %get-tuple-element.39.refs_0_, bf16[4,4,2,8,640]{4,3,2,1,0:T(8,128)(2,1)} %copy-done.6, ...), custom_call_target="tpu_custom_call" | custom-call | tf_op jit(solution)/shard_map/pallas_call | solution.py:63
  170.2 4.0 %collective-permute-start.6 = (bf16[4,4,2,8,640]{4,3,2,1,0:T(8,128)(2,1)}, bf16[4,4,2,8,640]{4,3,2,1,0:T(8,128)(2,1)S(1)}, u32[]{:S(2)}, u32[]{:S(2)}) collective-permute-start(bf16[4,4,2,8,640]{4,3,2,1,0:T(8,128)(2,1)} %get-tuple-element.9), channel_id=1, source_target_pairs={{0,768},{64,832},{128,896},{192,960},{256,0},{320,64},{384,128},{4... | collective-permute-start | bytes 983048 | tf_op jit(solution)/shard_map/ppermute | solution.py:80
  174.2 3.3 %collective-permute-start.7 = (bf16[4,4,2,8,640]{4,3,2,1,0:T(8,128)(2,1)}, bf16[4,4,2,8,640]{4,3,2,1,0:T(8,128)(2,1)S(1)}, u32[]{:S(2)}, u32[]{:S(2)}) collective-permute-start(bf16[4,4,2,8,640]{4,3,2,1,0:T(8,128)(2,1)} %get-tuple-element.10), channel_id=1, source_target_pairs={{0,512},{64,576},{128,640},{192,704},{256,768},{320,832},{384,896}... | collective-permute-start | bytes 983048 | tf_op jit(solution)/shard_map/ppermute | solution.py:80
  181.6 4.7 %collective-permute-done.7 = bf16[4,4,2,8,640]{4,3,2,1,0:T(8,128)(2,1)S(1)} collective-permute-done((bf16[4,4,2,8,640]{4,3,2,1,0:T(8,128)(2,1)}, bf16[4,4,2,8,640]{4,3,2,1,0:T(8,128)(2,1)S(1)}, u32[]{:S(2)}, u32[]{:S(2)}) %collective-permute-start.7) | collective-permute-done | bytes 327712 | tf_op jit(solution)/shard_map/ppermute | solution.py:80
  186.3 8.1 %collective-permute-done.8 = bf16[4,4,2,8,640]{4,3,2,1,0:T(8,128)(2,1)S(1)} collective-permute-done((bf16[4,4,2,8,640]{4,3,2,1,0:T(8,128)(2,1)}, bf16[4,4,2,8,640]{4,3,2,1,0:T(8,128)(2,1)S(1)}, u32[]{:S(2)}, u32[]{:S(2)}) %collective-permute-start.8) | collective-permute-done | bytes 327712 | tf_op jit(solution)/shard_map/ppermute | solution.py:80
  194.6 10.9 %collective-permute-start.9 = (bf16[4,4,2,8,640]{4,3,2,1,0:T(8,128)(2,1)S(1)}, bf16[4,4,2,8,640]{4,3,2,1,0:T(8,128)(2,1)S(1)}, u32[]{:S(2)}, u32[]{:S(2)}) collective-permute-start(bf16[4,4,2,8,640]{4,3,2,1,0:T(8,128)(2,1)S(1)} %pad_maximum_fusion.6), channel_id=1, source_target_pairs={{0,192},{64,0},{128,64},{192,128},{256,448},{320,256},{384,320},{4... | collective-permute-start | bytes 983048 | tf_op jit(solution)/shard_map/ppermute | solution.py:80
  205.5 3.1 %collective-permute-start.10 = (bf16[4,4,2,8,640]{4,3,2,1,0:T(8,128)(2,1)S(1)}, bf16[4,4,2,8,640]{4,3,2,1,0:T(8,128)(2,1)S(1)}, u32[]{:S(2)}, u32[]{:S(2)}) collective-permute-start(bf16[4,4,2,8,640]{4,3,2,1,0:T(8,128)(2,1)S(1)} %pad_maximum_fusion.7), channel_id=1, source_target_pairs={{0,128},{64,192},{128,0},{192,64},{256,384},{320,448},{384,256},{4... | collective-permute-start | bytes 983048 | tf_op jit(solution)/shard_map/ppermute | solution.py:80
  209.4 7.1 %collective-permute-start.11 = (bf16[4,4,2,8,640]{4,3,2,1,0:T(8,128)(2,1)}, bf16[4,4,2,8,640]{4,3,2,1,0:T(8,128)(2,1)S(1)}, u32[]{:S(2)}, u32[]{:S(2)}) collective-permute-start(bf16[4,4,2,8,640]{4,3,2,1,0:T(8,128)(2,1)} %pad_maximum_fusion.8), channel_id=1, source_target_pairs={{0,64},{64,128},{128,192},{192,0},{256,320},{320,384},{384,448},{4... | collective-permute-start | bytes 983048 | tf_op jit(solution)/shard_map/ppermute | solution.py:80
  216.7 20.5 %collective-permute-done.9 = bf16[4,4,2,8,640]{4,3,2,1,0:T(8,128)(2,1)S(1)} collective-permute-done((bf16[4,4,2,8,640]{4,3,2,1,0:T(8,128)(2,1)S(1)}, bf16[4,4,2,8,640]{4,3,2,1,0:T(8,128)(2,1)S(1)}, u32[]{:S(2)}, u32[]{:S(2)}) %collective-permute-start.9) | collective-permute-done | bytes 327712 | tf_op jit(solution)/shard_map/ppermute | solution.py:80
  237.2 20.9 %collective-permute-done.10 = bf16[4,4,2,8,640]{4,3,2,1,0:T(8,128)(2,1)S(1)} collective-permute-done((bf16[4,4,2,8,640]{4,3,2,1,0:T(8,128)(2,1)S(1)}, bf16[4,4,2,8,640]{4,3,2,1,0:T(8,128)(2,1)S(1)}, u32[]{:S(2)}, u32[]{:S(2)}) %collective-permute-start.10) | collective-permute-done | bytes 327712 | tf_op jit(solution)/shard_map/ppermute | solution.py:80
  (59 shorter events, 17.3 us)
Async XLA Ops:
  52.8 8.1 %copy-start = (bf16[8,8,4,640]{3,2,1,0:T(4,128)(2,1)S(1)}, bf16[8,8,4,640]{3,2,1,0:T(4,128)(2,1)}, u32[]{:S(2)}) copy-start(bf16[8,8,4,640]{3,2,1,0:T(4,128)(2,1)} %param.4) | copy-start | bytes 983044
  52.8 8.1 %copy-start.1 = (bf16[8,8,4,640]{3,2,1,0:T(4,128)(2,1)S(1)}, bf16[8,8,4,640]{3,2,1,0:T(4,128)(2,1)}, u32[]{:S(2)}) copy-start(bf16[8,8,4,640]{3,2,1,0:T(4,128)(2,1)} %param.5) | copy-start | bytes 983044
  52.8 206.3 %all-to-all-start.1 = ((bf16[64,4,1,4,640]{4,3,2,1,0:T(4,128)(2,1)}), bf16[64,4,1,4,640]{4,3,2,1,0:T(4,128)(2,1)S(1)}, u32[]{:S(2)}, u32[]{:S(2)}) async-start(bf16[64,4,1,4,640]{4,3,2,1,0:T(4,128)(2,1)} %shard_map.75), calls=%async_computation.1 | async-start | bytes 2621440 | tf_op jit(solution)/shard_map/all_to_all | solution.py:92
  60.8 1.0 copy-start.2
  60.8 1.1 copy-start.3
  62.3 13.4 %collective-permute-start = (bf16[4,4,2,8,640]{4,3,2,1,0:T(8,128)(2,1)S(1)}, bf16[4,4,2,8,640]{4,3,2,1,0:T(8,128)(2,1)S(1)}, u32[]{:S(2)}, u32[]{:S(2)}) collective-permute-start(bf16[4,4,2,8,640]{4,3,2,1,0:T(8,128)(2,1)S(1)} %bitcast.117), channel_id=1, source_target_pairs={{0,256},{64,320},{128,384},{192,448},{256,512},{320,576},{384,640}... | collective-permute-start | bytes 983048 | tf_op jit(solution)/shard_map/ppermute | solution.py:80
  65.9 16.9 %collective-permute-start.1 = (bf16[4,4,2,8,640]{4,3,2,1,0:T(8,128)(2,1)}, bf16[4,4,2,8,640]{4,3,2,1,0:T(8,128)(2,1)S(1)}, u32[]{:S(2)}, u32[]{:S(2)}) collective-permute-start(bf16[4,4,2,8,640]{4,3,2,1,0:T(8,128)(2,1)} %bitcast.90), channel_id=1, source_target_pairs={{0,512},{64,576},{128,640},{192,704},{256,768},{320,832},{384,896}... | collective-permute-start | bytes 983048 | tf_op jit(solution)/shard_map/ppermute | solution.py:80
  71.6 14.8 %collective-permute-start.2 = (bf16[4,4,2,8,640]{4,3,2,1,0:T(8,128)(2,1)}, bf16[4,4,2,8,640]{4,3,2,1,0:T(8,128)(2,1)S(1)}, u32[]{:S(2)}, u32[]{:S(2)}) collective-permute-start(bf16[4,4,2,8,640]{4,3,2,1,0:T(8,128)(2,1)} %bitcast.89), channel_id=1, source_target_pairs={{0,768},{64,832},{128,896},{192,960},{256,0},{320,64},{384,128},{4... | collective-permute-start | bytes 983048 | tf_op jit(solution)/shard_map/ppermute | solution.py:80
  87.4 30.3 %collective-permute-start.5 = (bf16[4,4,2,8,640]{4,3,2,1,0:T(8,128)(2,1)S(1)}, bf16[4,4,2,8,640]{4,3,2,1,0:T(8,128)(2,1)S(1)}, u32[]{:S(2)}, u32[]{:S(2)}) collective-permute-start(bf16[4,4,2,8,640]{4,3,2,1,0:T(8,128)(2,1)S(1)} %get-tuple-element.36), channel_id=1, source_target_pairs={{0,192},{64,0},{128,64},{192,128},{256,448},{320,256},{384,320},{4... | collective-permute-start | bytes 983048 | tf_op jit(solution)/shard_map/ppermute | solution.py:80
  100.9 50.6 %collective-permute-start.4 = (bf16[4,4,2,8,640]{4,3,2,1,0:T(8,128)(2,1)S(1)}, bf16[4,4,2,8,640]{4,3,2,1,0:T(8,128)(2,1)S(1)}, u32[]{:S(2)}, u32[]{:S(2)}) collective-permute-start(bf16[4,4,2,8,640]{4,3,2,1,0:T(8,128)(2,1)S(1)} %get-tuple-element.37), channel_id=1, source_target_pairs={{0,128},{64,192},{128,0},{192,64},{256,384},{320,448},{384,256},{4... | collective-permute-start | bytes 983048 | tf_op jit(solution)/shard_map/ppermute | solution.py:80
  104.0 57.6 %collective-permute-start.3 = (bf16[4,4,2,8,640]{4,3,2,1,0:T(8,128)(2,1)S(1)}, bf16[4,4,2,8,640]{4,3,2,1,0:T(8,128)(2,1)S(1)}, u32[]{:S(2)}, u32[]{:S(2)}) collective-permute-start(bf16[4,4,2,8,640]{4,3,2,1,0:T(8,128)(2,1)S(1)} %get-tuple-element.38), channel_id=1, source_target_pairs={{0,64},{64,128},{128,192},{192,0},{256,320},{320,384},{384,448},{4... | collective-permute-start | bytes 983048 | tf_op jit(solution)/shard_map/ppermute | solution.py:80
  117.7 43.9 %copy-start.4 = (bf16[4,4,2,8,640]{4,3,2,1,0:T(8,128)(2,1)}, bf16[4,4,2,8,640]{4,3,2,1,0:T(8,128)(2,1)S(1)}, u32[]{:S(2)}) copy-start(bf16[4,4,2,8,640]{4,3,2,1,0:T(8,128)(2,1)S(1)} %collective-permute-done.5.refs_3_) | copy-start | bytes 983044
  151.5 10.1 %copy-start.5 = (bf16[4,4,2,8,640]{4,3,2,1,0:T(8,128)(2,1)}, bf16[4,4,2,8,640]{4,3,2,1,0:T(8,128)(2,1)S(1)}, u32[]{:S(2)}) copy-start(bf16[4,4,2,8,640]{4,3,2,1,0:T(8,128)(2,1)S(1)} %collective-permute-done.4.refs_2_) | copy-start | bytes 983044
  161.6 0.7 copy-start.6
  170.2 11.4 %collective-permute-start.6 = (bf16[4,4,2,8,640]{4,3,2,1,0:T(8,128)(2,1)}, bf16[4,4,2,8,640]{4,3,2,1,0:T(8,128)(2,1)S(1)}, u32[]{:S(2)}, u32[]{:S(2)}) collective-permute-start(bf16[4,4,2,8,640]{4,3,2,1,0:T(8,128)(2,1)} %get-tuple-element.9), channel_id=1, source_target_pairs={{0,768},{64,832},{128,896},{192,960},{256,0},{320,64},{384,128},{4... | collective-permute-start | bytes 983048 | tf_op jit(solution)/shard_map/ppermute | solution.py:80
  174.2 12.1 %collective-permute-start.7 = (bf16[4,4,2,8,640]{4,3,2,1,0:T(8,128)(2,1)}, bf16[4,4,2,8,640]{4,3,2,1,0:T(8,128)(2,1)S(1)}, u32[]{:S(2)}, u32[]{:S(2)}) collective-permute-start(bf16[4,4,2,8,640]{4,3,2,1,0:T(8,128)(2,1)} %get-tuple-element.10), channel_id=1, source_target_pairs={{0,512},{64,576},{128,640},{192,704},{256,768},{320,832},{384,896}... | collective-permute-start | bytes 983048 | tf_op jit(solution)/shard_map/ppermute | solution.py:80
  178.6 15.9 %collective-permute-start.8 = (bf16[4,4,2,8,640]{4,3,2,1,0:T(8,128)(2,1)}, bf16[4,4,2,8,640]{4,3,2,1,0:T(8,128)(2,1)S(1)}, u32[]{:S(2)}, u32[]{:S(2)}) collective-permute-start(bf16[4,4,2,8,640]{4,3,2,1,0:T(8,128)(2,1)} %get-tuple-element.11), channel_id=1, source_target_pairs={{0,256},{64,320},{128,384},{192,448},{256,512},{320,576},{384,640}... | collective-permute-start | bytes 983048 | tf_op jit(solution)/shard_map/ppermute | solution.py:80
  194.6 42.6 %collective-permute-start.9 = (bf16[4,4,2,8,640]{4,3,2,1,0:T(8,128)(2,1)S(1)}, bf16[4,4,2,8,640]{4,3,2,1,0:T(8,128)(2,1)S(1)}, u32[]{:S(2)}, u32[]{:S(2)}) collective-permute-start(bf16[4,4,2,8,640]{4,3,2,1,0:T(8,128)(2,1)S(1)} %pad_maximum_fusion.6), channel_id=1, source_target_pairs={{0,192},{64,0},{128,64},{192,128},{256,448},{320,256},{384,320},{4... | collective-permute-start | bytes 983048 | tf_op jit(solution)/shard_map/ppermute | solution.py:80
  205.5 52.6 %collective-permute-start.10 = (bf16[4,4,2,8,640]{4,3,2,1,0:T(8,128)(2,1)S(1)}, bf16[4,4,2,8,640]{4,3,2,1,0:T(8,128)(2,1)S(1)}, u32[]{:S(2)}, u32[]{:S(2)}) collective-permute-start(bf16[4,4,2,8,640]{4,3,2,1,0:T(8,128)(2,1)S(1)} %pad_maximum_fusion.7), channel_id=1, source_target_pairs={{0,128},{64,192},{128,0},{192,64},{256,384},{320,448},{384,256},{4... | collective-permute-start | bytes 983048 | tf_op jit(solution)/shard_map/ppermute | solution.py:80
  209.4 48.7 %collective-permute-start.11 = (bf16[4,4,2,8,640]{4,3,2,1,0:T(8,128)(2,1)}, bf16[4,4,2,8,640]{4,3,2,1,0:T(8,128)(2,1)S(1)}, u32[]{:S(2)}, u32[]{:S(2)}) collective-permute-start(bf16[4,4,2,8,640]{4,3,2,1,0:T(8,128)(2,1)} %pad_maximum_fusion.8), channel_id=1, source_target_pairs={{0,64},{64,128},{128,192},{192,0},{256,320},{320,384},{384,448},{4... | collective-permute-start | bytes 983048 | tf_op jit(solution)/shard_map/ppermute | solution.py:80

commit v4 on v3

--- a/solution.py
+++ b/solution.py
@@ -58,13 +58,15 @@
             attend(x_refs, o_refs, item, pl.ds(pair * HEAD_PAIR, HEAD_PAIR))
 
 
-def attention(pieces):
+def attention(pieces, near_core):
     spec = pl.BlockSpec(memory_space=pltpu.VMEM)
+    if near_core:
+        pieces = [pltpu.with_memory_space_constraint(p, pltpu.VMEM) for p in pieces]
     return pl.pallas_call(
         attention_kernel,
         in_specs=[spec] * len(pieces),
         out_specs=[spec] * len(pieces),
-        out_shape=[jax.ShapeDtypeStruct(p.shape, p.dtype) for p in pieces],
+        out_shape=[pltpu.VMEM(p.shape, p.dtype) if near_core else jax.ShapeDtypeStruct(p.shape, p.dtype) for p in pieces],
     )(*pieces)
 
 
@@ -97,9 +99,9 @@
     send = send.reshape((FACTOR, FACTOR) + send.shape[1:])
     turned = jnp.stack([shift(pick(send, near + m), False, m) for m in range(FACTOR)], axis=1)
     lat_got = [shift(pick(turned, far + k), True, k) for k in range(FACTOR)]
-    (lon_done,) = attention([lon_got])
+    (lon_done,) = attention([lon_got], False)
     lon_back = swap_lon(lon_done)
-    lat_done = attention(lat_got)
+    lat_done = attention(lat_got, True)
     back = [shift(lat_done[m], False, -m) for m in range(FACTOR)]
     home = [shift(jnp.stack([b[k] for b in back], axis=0), True, -k) for k in range(FACTOR)]
     lat_back = jnp.stack([pick(jnp.stack(home, axis=0), z - far) for z in range(FACTOR)], axis=1)

time: 264 us -> 261 us (0.989)
  the two profiles are of different devices: /device:TPU:205 before, /device:TPU:201 now
where the time goes in v4:
time: 261 us
  waiting for transfers between devices  119 us (46%)
  starting transfers between devices  70.3 us (27%)
  blocking collectives  47.1 us (18%)
  Pallas kernels  12.1 us (5%)
  local copies, waits for them, and re-layouts  7.03 us (3%)
  other arithmetic  3.95 us (2%)
    ppermute x12, waiting for transfers between devices, shift(): return lax.ppermute(piece, 'lat', pairs)  119 us
    ppermute x12, starting transfers between devices, shift(): return lax.ppermute(piece, 'lat', pairs)  62.2 us
    all_to_all x1, blocking collectives, on_device(): lax.all_to_all(t, 'lon', split_axis=0, concat_axis=0, tiled=True)  47.1 us
    pallas_call x2, Pallas kernels, attention(): pl.pallas_call(attention_kernel, in_specs=[spec] * len(pieces), out_specs...  12.1 us
    all_to_all x1, starting transfers between devices, on_device(): lax.all_to_all(t, 'lon', split_axis=0, concat_axis=0, tiled=True)  8.11 us
  transfers between devices with their start and end apart: 13, of which 11 were waited for; matrix products, arithmetic and copies ran while one was open for 1% of the time, Pallas kernels for 2%

profile of v4, /device:TPU:201, one launch (start us, length us, event | category | flops | bytes accessed | tf_op | source)
XLA Modules:
  0.0 260.8 jit_solution(3802087589801035658)
XLA Ops:
  0.6 2.3 pad_maximum_fusion
  2.9 47.1 %all_to_all.10.refs_0_ = bf16[64,4,1,4,640]{4,3,2,1,0:T(4,128)(2,1)} all-to-all(bf16[64,4,1,4,640]{4,3,2,1,0:T(4,128)(2,1)S(1)} %pad_maximum_fusion), channel_id=1, replica_groups=mesh['lat'=16,'lon'=64] {'lon'}, dimensions={0} | all-to-all | bytes 2621440 | tf_op jit(solution)/shard_map/all_to_all | solution.py:94
  50.0 6.5 %shard_map.75 = bf16[64,4,1,4,640]{4,3,2,1,0:T(4,128)(2,1)} custom-call(bf16[64,4,1,4,640]{4,3,2,1,0:T(4,128)(2,1)} %all_to_all.10.refs_0_), custom_call_target="tpu_custom_call" | custom-call | tf_op jit(solution)/shard_map/pallas_call | solution.py:65
  56.5 8.1 %all-to-all-start.1 = ((bf16[64,4,1,4,640]{4,3,2,1,0:T(4,128)(2,1)}), bf16[64,4,1,4,640]{4,3,2,1,0:T(4,128)(2,1)}, u32[]{:S(2)}, u32[]{:S(2)}) async-start(bf16[64,4,1,4,640]{4,3,2,1,0:T(4,128)(2,1)} %shard_map.75), calls=%async_computation.1 | async-start | bytes 2621440 | tf_op jit(solution)/shard_map/all_to_all | solution.py:94
  70.1 4.6 %collective-permute-start.2 = (bf16[4,4,2,8,640]{4,3,2,1,0:T(8,128)(2,1)S(1)}, bf16[4,4,2,8,640]{4,3,2,1,0:T(8,128)(2,1)S(1)}, u32[]{:S(2)}, u32[]{:S(2)}) collective-permute-start(bf16[4,4,2,8,640]{4,3,2,1,0:T(8,128)(2,1)S(1)} %bitcast.119), channel_id=1, source_target_pairs={{0,768},{64,832},{128,896},{192,960},{256,0},{320,64},{384,128},{4... | collective-permute-start | bytes 983048 | tf_op jit(solution)/shard_map/ppermute | solution.py:82
  74.8 10.4 %collective-permute-done = bf16[4,4,2,8,640]{4,3,2,1,0:T(8,128)(2,1)S(1)} collective-permute-done((bf16[4,4,2,8,640]{4,3,2,1,0:T(8,128)(2,1)S(1)}, bf16[4,4,2,8,640]{4,3,2,1,0:T(8,128)(2,1)S(1)}, u32[]{:S(2)}, u32[]{:S(2)}) %collective-permute-start) | collective-permute-done | bytes 327712 | tf_op jit(solution)/shard_map/ppermute | solution.py:82
  85.3 2.3 collective-permute-done.2
  87.9 11.5 %collective-permute-start.5 = (bf16[4,4,2,8,640]{4,3,2,1,0:T(8,128)(2,1)S(1)}, bf16[4,4,2,8,640]{4,3,2,1,0:T(8,128)(2,1)S(1)}, u32[]{:S(2)}, u32[]{:S(2)}) collective-permute-start(bf16[4,4,2,8,640]{4,3,2,1,0:T(8,128)(2,1)S(1)} %get-tuple-element.36), channel_id=1, source_target_pairs={{0,192},{64,0},{128,64},{192,128},{256,448},{320,256},{384,320},{4... | collective-permute-start | bytes 983048 | tf_op jit(solution)/shard_map/ppermute | solution.py:82
  99.4 3.1 %collective-permute-start.4 = (bf16[4,4,2,8,640]{4,3,2,1,0:T(8,128)(2,1)S(1)}, bf16[4,4,2,8,640]{4,3,2,1,0:T(8,128)(2,1)S(1)}, u32[]{:S(2)}, u32[]{:S(2)}) collective-permute-start(bf16[4,4,2,8,640]{4,3,2,1,0:T(8,128)(2,1)S(1)} %get-tuple-element.37), channel_id=1, source_target_pairs={{0,128},{64,192},{128,0},{192,64},{256,384},{320,448},{384,256},{4... | collective-permute-start | bytes 983048 | tf_op jit(solution)/shard_map/ppermute | solution.py:82
  102.5 7.5 %collective-permute-start.3 = (bf16[4,4,2,8,640]{4,3,2,1,0:T(8,128)(2,1)S(1)}, bf16[4,4,2,8,640]{4,3,2,1,0:T(8,128)(2,1)S(1)}, u32[]{:S(2)}, u32[]{:S(2)}) collective-permute-start(bf16[4,4,2,8,640]{4,3,2,1,0:T(8,128)(2,1)S(1)} %get-tuple-element.38), channel_id=1, source_target_pairs={{0,64},{64,128},{128,192},{192,0},{256,320},{320,384},{384,448},{4... | collective-permute-start | bytes 983048 | tf_op jit(solution)/shard_map/ppermute | solution.py:82
  110.0 6.2 %collective-permute-done.5.refs_3_ = bf16[4,4,2,8,640]{4,3,2,1,0:T(8,128)(2,1)S(1)} collective-permute-done((bf16[4,4,2,8,640]{4,3,2,1,0:T(8,128)(2,1)S(1)}, bf16[4,4,2,8,640]{4,3,2,1,0:T(8,128)(2,1)S(1)}, u32[]{:S(2)}, u32[]{:S(2)}) %collective-permute-start.5) | collective-permute-done | bytes 327712 | tf_op jit(solution)/shard_map/ppermute | solution.py:82
  116.2 22.5 %collective-permute-done.4.refs_2_ = bf16[4,4,2,8,640]{4,3,2,1,0:T(8,128)(2,1)S(1)} collective-permute-done((bf16[4,4,2,8,640]{4,3,2,1,0:T(8,128)(2,1)S(1)}, bf16[4,4,2,8,640]{4,3,2,1,0:T(8,128)(2,1)S(1)}, u32[]{:S(2)}, u32[]{:S(2)}) %collective-permute-start.4) | collective-permute-done | bytes 327712 | tf_op jit(solution)/shard_map/ppermute | solution.py:82
  138.7 21.5 %collective-permute-done.3.refs_1_ = bf16[4,4,2,8,640]{4,3,2,1,0:T(8,128)(2,1)S(1)} collective-permute-done((bf16[4,4,2,8,640]{4,3,2,1,0:T(8,128)(2,1)S(1)}, bf16[4,4,2,8,640]{4,3,2,1,0:T(8,128)(2,1)S(1)}, u32[]{:S(2)}, u32[]{:S(2)}) %collective-permute-start.3) | collective-permute-done | bytes 327712 | tf_op jit(solution)/shard_map/ppermute | solution.py:82
  160.2 5.6 %shard_map.76 = (bf16[4,4,2,8,640]{4,3,2,1,0:T(8,128)(2,1)S(1)}, bf16[4,4,2,8,640]{4,3,2,1,0:T(8,128)(2,1)S(1)}, bf16[4,4,2,8,640]{4,3,2,1,0:T(8,128)(2,1)S(1)}, bf16[4,4,2,8,640]{4,3,2,1,0:T(8,128)(2,1)S(1)}) custom-call(bf16[4,4,2,8,640]{4,3,2,1,0:T(8,128)(2,1)S(1)} %get-tuple-element.39.refs_0_, ...), custom_call_target="tpu_custom_call" | custom-call | tf_op jit(solution)/shard_map/pallas_call | solution.py:65
  165.7 5.3 %collective-permute-start.6 = (bf16[4,4,2,8,640]{4,3,2,1,0:T(8,128)(2,1)S(1)}, bf16[4,4,2,8,640]{4,3,2,1,0:T(8,128)(2,1)S(1)}, u32[]{:S(2)}, u32[]{:S(2)}) collective-permute-start(bf16[4,4,2,8,640]{4,3,2,1,0:T(8,128)(2,1)S(1)} %get-tuple-element.9), channel_id=1, source_target_pairs={{0,768},{64,832},{128,896},{192,960},{256,0},{320,64},{384,128},{4... | collective-permute-start | bytes 983048 | tf_op jit(solution)/shard_map/ppermute | solution.py:82
  171.0 3.4 %collective-permute-start.7 = (bf16[4,4,2,8,640]{4,3,2,1,0:T(8,128)(2,1)S(1)}, bf16[4,4,2,8,640]{4,3,2,1,0:T(8,128)(2,1)S(1)}, u32[]{:S(2)}, u32[]{:S(2)}) collective-permute-start(bf16[4,4,2,8,640]{4,3,2,1,0:T(8,128)(2,1)S(1)} %get-tuple-element.10), channel_id=1, source_target_pairs={{0,512},{64,576},{128,640},{192,704},{256,768},{320,832},{384,896}... | collective-permute-start | bytes 983048 | tf_op jit(solution)/shard_map/ppermute | solution.py:82
  174.5 1.9 collective-permute-start.8
  178.3 4.6 %collective-permute-done.7 = bf16[4,4,2,8,640]{4,3,2,1,0:T(8,128)(2,1)S(1)} collective-permute-done((bf16[4,4,2,8,640]{4,3,2,1,0:T(8,128)(2,1)S(1)}, bf16[4,4,2,8,640]{4,3,2,1,0:T(8,128)(2,1)S(1)}, u32[]{:S(2)}, u32[]{:S(2)}) %collective-permute-start.7) | collective-permute-done | bytes 327712 | tf_op jit(solution)/shard_map/ppermute | solution.py:82
  182.9 8.1 %collective-permute-done.8 = bf16[4,4,2,8,640]{4,3,2,1,0:T(8,128)(2,1)S(1)} collective-permute-done((bf16[4,4,2,8,640]{4,3,2,1,0:T(8,128)(2,1)S(1)}, bf16[4,4,2,8,640]{4,3,2,1,0:T(8,128)(2,1)S(1)}, u32[]{:S(2)}, u32[]{:S(2)}) %collective-permute-start.8) | collective-permute-done | bytes 327712 | tf_op jit(solution)/shard_map/ppermute | solution.py:82
  191.2 10.9 %collective-permute-start.9 = (bf16[4,4,2,8,640]{4,3,2,1,0:T(8,128)(2,1)S(1)}, bf16[4,4,2,8,640]{4,3,2,1,0:T(8,128)(2,1)S(1)}, u32[]{:S(2)}, u32[]{:S(2)}) collective-permute-start(bf16[4,4,2,8,640]{4,3,2,1,0:T(8,128)(2,1)S(1)} %pad_maximum_fusion.6), channel_id=1, source_target_pairs={{0,192},{64,0},{128,64},{192,128},{256,448},{320,256},{384,320},{4... | collective-permute-start | bytes 983048 | tf_op jit(solution)/shard_map/ppermute | solution.py:82
  202.1 3.1 %collective-permute-start.10 = (bf16[4,4,2,8,640]{4,3,2,1,0:T(8,128)(2,1)S(1)}, bf16[4,4,2,8,640]{4,3,2,1,0:T(8,128)(2,1)S(1)}, u32[]{:S(2)}, u32[]{:S(2)}) collective-permute-start(bf16[4,4,2,8,640]{4,3,2,1,0:T(8,128)(2,1)S(1)} %pad_maximum_fusion.7), channel_id=1, source_target_pairs={{0,128},{64,192},{128,0},{192,64},{256,384},{320,448},{384,256},{4... | collective-permute-start | bytes 983048 | tf_op jit(solution)/shard_map/ppermute | solution.py:82
  205.3 7.1 %collective-permute-start.11 = (bf16[4,4,2,8,640]{4,3,2,1,0:T(8,128)(2,1)S(1)}, bf16[4,4,2,8,640]{4,3,2,1,0:T(8,128)(2,1)S(1)}, u32[]{:S(2)}, u32[]{:S(2)}) collective-permute-start(bf16[4,4,2,8,640]{4,3,2,1,0:T(8,128)(2,1)S(1)} %pad_maximum_fusion.8), channel_id=1, source_target_pairs={{0,64},{64,128},{128,192},{192,0},{256,320},{320,384},{384,448},{4... | collective-permute-start | bytes 983048 | tf_op jit(solution)/shard_map/ppermute | solution.py:82
  212.6 20.0 %collective-permute-done.9 = bf16[4,4,2,8,640]{4,3,2,1,0:T(8,128)(2,1)S(1)} collective-permute-done((bf16[4,4,2,8,640]{4,3,2,1,0:T(8,128)(2,1)S(1)}, bf16[4,4,2,8,640]{4,3,2,1,0:T(8,128)(2,1)S(1)}, u32[]{:S(2)}, u32[]{:S(2)}) %collective-permute-start.9) | collective-permute-done | bytes 327712 | tf_op jit(solution)/shard_map/ppermute | solution.py:82
  232.6 21.2 %collective-permute-done.10 = bf16[4,4,2,8,640]{4,3,2,1,0:T(8,128)(2,1)S(1)} collective-permute-done((bf16[4,4,2,8,640]{4,3,2,1,0:T(8,128)(2,1)S(1)}, bf16[4,4,2,8,640]{4,3,2,1,0:T(8,128)(2,1)S(1)}, u32[]{:S(2)}, u32[]{:S(2)}) %collective-permute-start.10) | collective-permute-done | bytes 327712 | tf_op jit(solution)/shard_map/ppermute | solution.py:82
  (53 shorter events, 14.6 us)
Async XLA Ops:
  56.5 8.2 %copy-start = (bf16[8,8,4,640]{3,2,1,0:T(4,128)(2,1)S(1)}, bf16[8,8,4,640]{3,2,1,0:T(4,128)(2,1)}, u32[]{:S(2)}) copy-start(bf16[8,8,4,640]{3,2,1,0:T(4,128)(2,1)} %param.4) | copy-start | bytes 983044
  56.5 8.3 %copy-start.1 = (bf16[8,8,4,640]{3,2,1,0:T(4,128)(2,1)S(1)}, bf16[8,8,4,640]{3,2,1,0:T(4,128)(2,1)}, u32[]{:S(2)}) copy-start(bf16[8,8,4,640]{3,2,1,0:T(4,128)(2,1)} %param.5) | copy-start | bytes 983044
  56.5 198.6 %all-to-all-start.1 = ((bf16[64,4,1,4,640]{4,3,2,1,0:T(4,128)(2,1)}), bf16[64,4,1,4,640]{4,3,2,1,0:T(4,128)(2,1)}, u32[]{:S(2)}, u32[]{:S(2)}) async-start(bf16[64,4,1,4,640]{4,3,2,1,0:T(4,128)(2,1)} %shard_map.75), calls=%async_computation.1 | async-start | bytes 2621440 | tf_op jit(solution)/shard_map/all_to_all | solution.py:94
  64.6 1.0 copy-start.2
  64.6 1.1 copy-start.3
  66.2 19.1 %collective-permute-start = (bf16[4,4,2,8,640]{4,3,2,1,0:T(8,128)(2,1)S(1)}, bf16[4,4,2,8,640]{4,3,2,1,0:T(8,128)(2,1)S(1)}, u32[]{:S(2)}, u32[]{:S(2)}) collective-permute-start(bf16[4,4,2,8,640]{4,3,2,1,0:T(8,128)(2,1)S(1)} %bitcast.117), channel_id=1, source_target_pairs={{0,256},{64,320},{128,384},{192,448},{256,512},{320,576},{384,640}... | collective-permute-start | bytes 983048 | tf_op jit(solution)/shard_map/ppermute | solution.py:82
  68.1 17.1 %collective-permute-start.1 = (bf16[4,4,2,8,640]{4,3,2,1,0:T(8,128)(2,1)S(1)}, bf16[4,4,2,8,640]{4,3,2,1,0:T(8,128)(2,1)S(1)}, u32[]{:S(2)}, u32[]{:S(2)}) collective-permute-start(bf16[4,4,2,8,640]{4,3,2,1,0:T(8,128)(2,1)S(1)} %bitcast.118), channel_id=1, source_target_pairs={{0,512},{64,576},{128,640},{192,704},{256,768},{320,832},{384,896}... | collective-permute-start | bytes 983048 | tf_op jit(solution)/shard_map/ppermute | solution.py:82
  70.1 17.5 %collective-permute-start.2 = (bf16[4,4,2,8,640]{4,3,2,1,0:T(8,128)(2,1)S(1)}, bf16[4,4,2,8,640]{4,3,2,1,0:T(8,128)(2,1)S(1)}, u32[]{:S(2)}, u32[]{:S(2)}) collective-permute-start(bf16[4,4,2,8,640]{4,3,2,1,0:T(8,128)(2,1)S(1)} %bitcast.119), channel_id=1, source_target_pairs={{0,768},{64,832},{128,896},{192,960},{256,0},{320,64},{384,128},{4... | collective-permute-start | bytes 983048 | tf_op jit(solution)/shard_map/ppermute | solution.py:82
  87.9 28.3 %collective-permute-start.5 = (bf16[4,4,2,8,640]{4,3,2,1,0:T(8,128)(2,1)S(1)}, bf16[4,4,2,8,640]{4,3,2,1,0:T(8,128)(2,1)S(1)}, u32[]{:S(2)}, u32[]{:S(2)}) collective-permute-start(bf16[4,4,2,8,640]{4,3,2,1,0:T(8,128)(2,1)S(1)} %get-tuple-element.36), channel_id=1, source_target_pairs={{0,192},{64,0},{128,64},{192,128},{256,448},{320,256},{384,320},{4... | collective-permute-start | bytes 983048 | tf_op jit(solution)/shard_map/ppermute | solution.py:82
  99.4 39.2 %collective-permute-start.4 = (bf16[4,4,2,8,640]{4,3,2,1,0:T(8,128)(2,1)S(1)}, bf16[4,4,2,8,640]{4,3,2,1,0:T(8,128)(2,1)S(1)}, u32[]{:S(2)}, u32[]{:S(2)}) collective-permute-start(bf16[4,4,2,8,640]{4,3,2,1,0:T(8,128)(2,1)S(1)} %get-tuple-element.37), channel_id=1, source_target_pairs={{0,128},{64,192},{128,0},{192,64},{256,384},{320,448},{384,256},{4... | collective-permute-start | bytes 983048 | tf_op jit(solution)/shard_map/ppermute | solution.py:82
  102.5 57.6 %collective-permute-start.3 = (bf16[4,4,2,8,640]{4,3,2,1,0:T(8,128)(2,1)S(1)}, bf16[4,4,2,8,640]{4,3,2,1,0:T(8,128)(2,1)S(1)}, u32[]{:S(2)}, u32[]{:S(2)}) collective-permute-start(bf16[4,4,2,8,640]{4,3,2,1,0:T(8,128)(2,1)S(1)} %get-tuple-element.38), channel_id=1, source_target_pairs={{0,64},{64,128},{128,192},{192,0},{256,320},{320,384},{384,448},{4... | collective-permute-start | bytes 983048 | tf_op jit(solution)/shard_map/ppermute | solution.py:82
  165.7 12.6 %collective-permute-start.6 = (bf16[4,4,2,8,640]{4,3,2,1,0:T(8,128)(2,1)S(1)}, bf16[4,4,2,8,640]{4,3,2,1,0:T(8,128)(2,1)S(1)}, u32[]{:S(2)}, u32[]{:S(2)}) collective-permute-start(bf16[4,4,2,8,640]{4,3,2,1,0:T(8,128)(2,1)S(1)} %get-tuple-element.9), channel_id=1, source_target_pairs={{0,768},{64,832},{128,896},{192,960},{256,0},{320,64},{384,128},{4... | collective-permute-start | bytes 983048 | tf_op jit(solution)/shard_map/ppermute | solution.py:82
  171.0 11.9 %collective-permute-start.7 = (bf16[4,4,2,8,640]{4,3,2,1,0:T(8,128)(2,1)S(1)}, bf16[4,4,2,8,640]{4,3,2,1,0:T(8,128)(2,1)S(1)}, u32[]{:S(2)}, u32[]{:S(2)}) collective-permute-start(bf16[4,4,2,8,640]{4,3,2,1,0:T(8,128)(2,1)S(1)} %get-tuple-element.10), channel_id=1, source_target_pairs={{0,512},{64,576},{128,640},{192,704},{256,768},{320,832},{384,896}... | collective-permute-start | bytes 983048 | tf_op jit(solution)/shard_map/ppermute | solution.py:82
  174.5 16.6 %collective-permute-start.8 = (bf16[4,4,2,8,640]{4,3,2,1,0:T(8,128)(2,1)S(1)}, bf16[4,4,2,8,640]{4,3,2,1,0:T(8,128)(2,1)S(1)}, u32[]{:S(2)}, u32[]{:S(2)}) collective-permute-start(bf16[4,4,2,8,640]{4,3,2,1,0:T(8,128)(2,1)S(1)} %get-tuple-element.11), channel_id=1, source_target_pairs={{0,256},{64,320},{128,384},{192,448},{256,512},{320,576},{384,640}... | collective-permute-start | bytes 983048 | tf_op jit(solution)/shard_map/ppermute | solution.py:82
  191.2 41.5 %collective-permute-start.9 = (bf16[4,4,2,8,640]{4,3,2,1,0:T(8,128)(2,1)S(1)}, bf16[4,4,2,8,640]{4,3,2,1,0:T(8,128)(2,1)S(1)}, u32[]{:S(2)}, u32[]{:S(2)}) collective-permute-start(bf16[4,4,2,8,640]{4,3,2,1,0:T(8,128)(2,1)S(1)} %pad_maximum_fusion.6), channel_id=1, source_target_pairs={{0,192},{64,0},{128,64},{192,128},{256,448},{320,256},{384,320},{4... | collective-permute-start | bytes 983048 | tf_op jit(solution)/shard_map/ppermute | solution.py:82
  202.1 51.7 %collective-permute-start.10 = (bf16[4,4,2,8,640]{4,3,2,1,0:T(8,128)(2,1)S(1)}, bf16[4,4,2,8,640]{4,3,2,1,0:T(8,128)(2,1)S(1)}, u32[]{:S(2)}, u32[]{:S(2)}) collective-permute-start(bf16[4,4,2,8,640]{4,3,2,1,0:T(8,128)(2,1)S(1)} %pad_maximum_fusion.7), channel_id=1, source_target_pairs={{0,128},{64,192},{128,0},{192,64},{256,384},{320,448},{384,256},{4... | collective-permute-start | bytes 983048 | tf_op jit(solution)/shard_map/ppermute | solution.py:82
  205.3 48.7 %collective-permute-start.11 = (bf16[4,4,2,8,640]{4,3,2,1,0:T(8,128)(2,1)S(1)}, bf16[4,4,2,8,640]{4,3,2,1,0:T(8,128)(2,1)S(1)}, u32[]{:S(2)}, u32[]{:S(2)}) collective-permute-start(bf16[4,4,2,8,640]{4,3,2,1,0:T(8,128)(2,1)S(1)} %pad_maximum_fusion.8), channel_id=1, source_target_pairs={{0,64},{64,128},{128,192},{192,0},{256,320},{320,384},{384,448},{4... | collective-permute-start | bytes 983048 | tf_op jit(solution)/shard_map/ppermute | solution.py:82

commit v5 on v4

--- a/solution.py
+++ b/solution.py
@@ -70,6 +70,38 @@
     )(*pieces)
 
 
+def finish_kernel(places, lat_ref, lon_ref, *o_refs):
+    items, _, _ = lat_ref.shape[3:]
+    cols = lon_ref.shape[3]
+    first = pl.program_id(0) * (cols // items)
+    for t, o_ref in enumerate(o_refs):
+        lat_cols = []
+        for c in range(cols):
+            to = first + c // items
+            near = (to // FACTOR - places[0]) % FACTOR
+            far = (to % FACTOR - places[1]) % FACTOR
+            lat_cols.append(lat_ref[far, near, t, c % items].astype(jnp.float32))
+        lat_part = jnp.stack(lat_cols, axis=1)
+        o_ref[0] = (lon_ref[:, t, 0].astype(jnp.float32) + lat_part).astype(jnp.bfloat16)
+
+
+def finish(places, lat_back, lon_back, shape):
+    batch, rows, cols, feats = shape
+    tensors = lon_back.shape[1]
+    lat_back = pltpu.with_memory_space_constraint(lat_back, pltpu.VMEM)
+    return pl.pallas_call(
+        finish_kernel,
+        grid=(batch,),
+        in_specs=[
+            pl.BlockSpec(memory_space=pltpu.SMEM),
+            pl.BlockSpec(memory_space=pltpu.VMEM),
+            pl.BlockSpec((rows, tensors, 1, cols, feats), lambda b: (b, 0, 0, 0, 0)),
+        ],
+        out_specs=[pl.BlockSpec((1, rows, cols, feats), lambda b: (b, 0, 0, 0))] * tensors,
+        out_shape=[jax.ShapeDtypeStruct(shape, jnp.bfloat16)] * tensors,
+    )(places, lat_back, lon_back)
+
+
 def shift(piece, far, by):
     if by % FACTOR == 0:
         return piece
@@ -104,15 +136,9 @@
     lat_done = attention(lat_got, True)
     back = [shift(lat_done[m], False, -m) for m in range(FACTOR)]
     home = [shift(jnp.stack([b[k] for b in back], axis=0), True, -k) for k in range(FACTOR)]
-    lat_back = jnp.stack([pick(jnp.stack(home, axis=0), z - far) for z in range(FACTOR)], axis=1)
-    lat_back = jnp.stack([pick(lat_back, x - near) for x in range(FACTOR)], axis=0)
-    lat_back = lat_back.reshape((lat,) + lat_back.shape[2:])
-    results = []
-    for i in range(tensors):
-        a = lon_back[:, i].reshape(batch, rows, cols, feats)
-        b = lat_back[:, i].reshape(batch, cols, rows, feats).transpose(0, 2, 1, 3)
-        results.append((a.astype(jnp.float32) + b.astype(jnp.float32)).astype(jnp.bfloat16))
-    return tuple(results)
+    places = jnp.stack([near, far]).astype(jnp.int32)
+    rows_back = lon_back.transpose(0, 2, 1, 3, 4).reshape(batch * rows, tensors, 1, cols, feats)
+    return finish(places, jnp.stack(home, axis=0), rows_back, inputs[0].shape)
 
 
 def solution(mesh):

time: 261 us -> 262 us (level)
  the two profiles are of different devices: /device:TPU:201 before, /device:TPU:208 now
where the time goes in v5:
time: 262 us; the launch traced here: 261 us
  waiting for transfers between devices  116 us (44%)
  starting transfers between devices  73 us (28%)
  blocking collectives  46.8 us (18%)
  Pallas kernels  18.5 us (7%)
  other arithmetic  3.65 us (1%)
    ppermute x12, waiting for transfers between devices, shift(): return lax.ppermute(piece, 'lat', pairs)  116 us
    ppermute x12, starting transfers between devices, shift(): return lax.ppermute(piece, 'lat', pairs)  65 us
    all_to_all x1, blocking collectives, on_device(): lax.all_to_all(t, 'lon', split_axis=0, concat_axis=0, tiled=True)  46.8 us
    pallas_call x2, Pallas kernels, attention(): pl.pallas_call(attention_kernel, in_specs=[spec] * len(pieces), out_specs...  12.1 us
    all_to_all x1, starting transfers between devices, on_device(): lax.all_to_all(t, 'lon', split_axis=0, concat_axis=0, tiled=True)  8.03 us
    pallas_call x1, Pallas kernels, finish(): pl.pallas_call(finish_kernel, grid=(batch,), in_specs=[pl.BlockSpec(memor...  6.38 us
  transfers between devices with their start and end apart: 13, of which 9 were waited for; matrix products, arithmetic and copies ran while one was open for 1% of the time, Pallas kernels for 2%

profile of v5, /device:TPU:208, one launch (start us, length us, event | category | flops | bytes accessed | tf_op | source)
XLA Modules:
  0.0 261.0 jit_solution(13844269581455341180)
XLA Ops:
  2.9 46.8 %all_to_all.10.refs_0_ = bf16[64,4,1,4,640]{4,3,2,1,0:T(4,128)(2,1)} all-to-all(bf16[64,4,1,4,640]{4,3,2,1,0:T(4,128)(2,1)S(1)} %pad_maximum_fusion.3), channel_id=1, replica_groups=mesh['lat'=16,'lon'=64] {'lon'}, dimensions={0} | all-to-all | bytes 2621440 | tf_op jit(solution)/shard_map/all_to_all | solution.py:126
  49.7 6.5 %shard_map.76 = bf16[64,4,1,4,640]{4,3,2,1,0:T(4,128)(2,1)} custom-call(bf16[64,4,1,4,640]{4,3,2,1,0:T(4,128)(2,1)} %all_to_all.10.refs_0_), custom_call_target="tpu_custom_call" | custom-call | tf_op jit(solution)/shard_map/pallas_call | solution.py:65
  56.2 8.0 %all-to-all-start.1 = ((bf16[64,4,1,4,640]{4,3,2,1,0:T(4,128)(2,1)}), bf16[64,4,1,4,640]{4,3,2,1,0:T(4,128)(2,1)}, u32[]{:S(2)}, u32[]{:S(2)}) async-start(bf16[64,4,1,4,640]{4,3,2,1,0:T(4,128)(2,1)} %shard_map.76), calls=%async_computation.1 | async-start | bytes 2621440 | tf_op jit(solution)/shard_map/all_to_all | solution.py:126
  67.7 2.4 collective-permute-start.1
  70.2 4.6 %collective-permute-start.2 = (bf16[4,4,2,8,640]{4,3,2,1,0:T(8,128)(2,1)S(1)}, bf16[4,4,2,8,640]{4,3,2,1,0:T(8,128)(2,1)S(1)}, u32[]{:S(2)}, u32[]{:S(2)}) collective-permute-start(bf16[4,4,2,8,640]{4,3,2,1,0:T(8,128)(2,1)S(1)} %bitcast.63), channel_id=1, source_target_pairs={{0,768},{64,832},{128,896},{192,960},{256,0},{320,64},{384,128},{4... | collective-permute-start | bytes 983048 | tf_op jit(solution)/shard_map/ppermute | solution.py:114
  75.0 10.6 %collective-permute-done = bf16[4,4,2,8,640]{4,3,2,1,0:T(8,128)(2,1)S(1)} collective-permute-done((bf16[4,4,2,8,640]{4,3,2,1,0:T(8,128)(2,1)S(1)}, bf16[4,4,2,8,640]{4,3,2,1,0:T(8,128)(2,1)S(1)}, u32[]{:S(2)}, u32[]{:S(2)}) %collective-permute-start) | collective-permute-done | bytes 327712 | tf_op jit(solution)/shard_map/ppermute | solution.py:114
  85.6 2.6 collective-permute-done.2
  88.5 11.8 %collective-permute-start.5 = (bf16[4,4,2,8,640]{4,3,2,1,0:T(8,128)(2,1)S(1)}, bf16[4,4,2,8,640]{4,3,2,1,0:T(8,128)(2,1)S(1)}, u32[]{:S(2)}, u32[]{:S(2)}) collective-permute-start(bf16[4,4,2,8,640]{4,3,2,1,0:T(8,128)(2,1)S(1)} %get-tuple-element.12), channel_id=1, source_target_pairs={{0,192},{64,0},{128,64},{192,128},{256,448},{320,256},{384,320},{4... | collective-permute-start | bytes 983048 | tf_op jit(solution)/shard_map/ppermute | solution.py:114
  100.4 3.1 %collective-permute-start.4 = (bf16[4,4,2,8,640]{4,3,2,1,0:T(8,128)(2,1)S(1)}, bf16[4,4,2,8,640]{4,3,2,1,0:T(8,128)(2,1)S(1)}, u32[]{:S(2)}, u32[]{:S(2)}) collective-permute-start(bf16[4,4,2,8,640]{4,3,2,1,0:T(8,128)(2,1)S(1)} %get-tuple-element.13), channel_id=1, source_target_pairs={{0,128},{64,192},{128,0},{192,64},{256,384},{320,448},{384,256},{4... | collective-permute-start | bytes 983048 | tf_op jit(solution)/shard_map/ppermute | solution.py:114
  103.5 8.0 %collective-permute-start.3 = (bf16[4,4,2,8,640]{4,3,2,1,0:T(8,128)(2,1)S(1)}, bf16[4,4,2,8,640]{4,3,2,1,0:T(8,128)(2,1)S(1)}, u32[]{:S(2)}, u32[]{:S(2)}) collective-permute-start(bf16[4,4,2,8,640]{4,3,2,1,0:T(8,128)(2,1)S(1)} %get-tuple-element.14), channel_id=1, source_target_pairs={{0,64},{64,128},{128,192},{192,0},{256,320},{320,384},{384,448},{4... | collective-permute-start | bytes 983048 | tf_op jit(solution)/shard_map/ppermute | solution.py:114
  111.5 9.5 %collective-permute-done.5.refs_3_ = bf16[4,4,2,8,640]{4,3,2,1,0:T(8,128)(2,1)S(1)} collective-permute-done((bf16[4,4,2,8,640]{4,3,2,1,0:T(8,128)(2,1)S(1)}, bf16[4,4,2,8,640]{4,3,2,1,0:T(8,128)(2,1)S(1)}, u32[]{:S(2)}, u32[]{:S(2)}) %collective-permute-start.5) | collective-permute-done | bytes 327712 | tf_op jit(solution)/shard_map/ppermute | solution.py:114
  121.0 25.5 %collective-permute-done.4.refs_2_ = bf16[4,4,2,8,640]{4,3,2,1,0:T(8,128)(2,1)S(1)} collective-permute-done((bf16[4,4,2,8,640]{4,3,2,1,0:T(8,128)(2,1)S(1)}, bf16[4,4,2,8,640]{4,3,2,1,0:T(8,128)(2,1)S(1)}, u32[]{:S(2)}, u32[]{:S(2)}) %collective-permute-start.4) | collective-permute-done | bytes 327712 | tf_op jit(solution)/shard_map/ppermute | solution.py:114
  146.5 13.4 %collective-permute-done.3.refs_1_ = bf16[4,4,2,8,640]{4,3,2,1,0:T(8,128)(2,1)S(1)} collective-permute-done((bf16[4,4,2,8,640]{4,3,2,1,0:T(8,128)(2,1)S(1)}, bf16[4,4,2,8,640]{4,3,2,1,0:T(8,128)(2,1)S(1)}, u32[]{:S(2)}, u32[]{:S(2)}) %collective-permute-start.3) | collective-permute-done | bytes 327712 | tf_op jit(solution)/shard_map/ppermute | solution.py:114
  159.9 5.6 %shard_map.75 = (bf16[4,4,2,8,640]{4,3,2,1,0:T(8,128)(2,1)S(1)}, bf16[4,4,2,8,640]{4,3,2,1,0:T(8,128)(2,1)S(1)}, bf16[4,4,2,8,640]{4,3,2,1,0:T(8,128)(2,1)S(1)}, bf16[4,4,2,8,640]{4,3,2,1,0:T(8,128)(2,1)S(1)}) custom-call(bf16[4,4,2,8,640]{4,3,2,1,0:T(8,128)(2,1)S(1)} %get-tuple-element.15.refs_0_, ...), custom_call_target="tpu_custom_call" | custom-call | tf_op jit(solution)/shard_map/pallas_call | solution.py:65
  165.5 5.6 %collective-permute-start.6 = (bf16[4,4,2,8,640]{4,3,2,1,0:T(8,128)(2,1)S(1)}, bf16[4,4,2,8,640]{4,3,2,1,0:T(8,128)(2,1)S(1)}, u32[]{:S(2)}, u32[]{:S(2)}) collective-permute-start(bf16[4,4,2,8,640]{4,3,2,1,0:T(8,128)(2,1)S(1)} %get-tuple-element.9), channel_id=1, source_target_pairs={{0,768},{64,832},{128,896},{192,960},{256,0},{320,64},{384,128},{4... | collective-permute-start | bytes 983048 | tf_op jit(solution)/shard_map/ppermute | solution.py:114
  171.1 3.7 %collective-permute-start.7 = (bf16[4,4,2,8,640]{4,3,2,1,0:T(8,128)(2,1)S(1)}, bf16[4,4,2,8,640]{4,3,2,1,0:T(8,128)(2,1)S(1)}, u32[]{:S(2)}, u32[]{:S(2)}) collective-permute-start(bf16[4,4,2,8,640]{4,3,2,1,0:T(8,128)(2,1)S(1)} %get-tuple-element.10), channel_id=1, source_target_pairs={{0,512},{64,576},{128,640},{192,704},{256,768},{320,832},{384,896}... | collective-permute-start | bytes 983048 | tf_op jit(solution)/shard_map/ppermute | solution.py:114
  176.7 8.4 %collective-permute-done.6 = bf16[4,4,2,8,640]{4,3,2,1,0:T(8,128)(2,1)S(1)} collective-permute-done((bf16[4,4,2,8,640]{4,3,2,1,0:T(8,128)(2,1)S(1)}, bf16[4,4,2,8,640]{4,3,2,1,0:T(8,128)(2,1)S(1)}, u32[]{:S(2)}, u32[]{:S(2)}) %collective-permute-start.6) | collective-permute-done | bytes 327712 | tf_op jit(solution)/shard_map/ppermute | solution.py:114
  185.3 5.5 %collective-permute-done.8 = bf16[4,4,2,8,640]{4,3,2,1,0:T(8,128)(2,1)S(1)} collective-permute-done((bf16[4,4,2,8,640]{4,3,2,1,0:T(8,128)(2,1)S(1)}, bf16[4,4,2,8,640]{4,3,2,1,0:T(8,128)(2,1)S(1)}, u32[]{:S(2)}, u32[]{:S(2)}) %collective-permute-start.8) | collective-permute-done | bytes 327712 | tf_op jit(solution)/shard_map/ppermute | solution.py:114
  190.9 11.2 %collective-permute-start.9 = (bf16[4,4,2,8,640]{4,3,2,1,0:T(8,128)(2,1)S(1)}, bf16[4,4,2,8,640]{4,3,2,1,0:T(8,128)(2,1)S(1)}, u32[]{:S(2)}, u32[]{:S(2)}) collective-permute-start(bf16[4,4,2,8,640]{4,3,2,1,0:T(8,128)(2,1)S(1)} %pad_maximum_fusion.4), channel_id=1, source_target_pairs={{0,192},{64,0},{128,64},{192,128},{256,448},{320,256},{384,320},{4... | collective-permute-start | bytes 983048 | tf_op jit(solution)/shard_map/ppermute | solution.py:114
  202.1 3.4 %collective-permute-start.10 = (bf16[4,4,2,8,640]{4,3,2,1,0:T(8,128)(2,1)S(1)}, bf16[4,4,2,8,640]{4,3,2,1,0:T(8,128)(2,1)S(1)}, u32[]{:S(2)}, u32[]{:S(2)}) collective-permute-start(bf16[4,4,2,8,640]{4,3,2,1,0:T(8,128)(2,1)S(1)} %pad_maximum_fusion.5), channel_id=1, source_target_pairs={{0,128},{64,192},{128,0},{192,64},{256,384},{320,448},{384,256},{4... | collective-permute-start | bytes 983048 | tf_op jit(solution)/shard_map/ppermute | solution.py:114
  205.6 7.3 %collective-permute-start.11 = (bf16[4,4,2,8,640]{4,3,2,1,0:T(8,128)(2,1)S(1)}, bf16[4,4,2,8,640]{4,3,2,1,0:T(8,128)(2,1)S(1)}, u32[]{:S(2)}, u32[]{:S(2)}) collective-permute-start(bf16[4,4,2,8,640]{4,3,2,1,0:T(8,128)(2,1)S(1)} %pad_maximum_fusion.6), channel_id=1, source_target_pairs={{0,64},{64,128},{128,192},{192,0},{256,320},{320,384},{384,448},{4... | collective-permute-start | bytes 983048 | tf_op jit(solution)/shard_map/ppermute | solution.py:114
  213.5 20.9 %collective-permute-done.9 = bf16[4,4,2,8,640]{4,3,2,1,0:T(8,128)(2,1)S(1)} collective-permute-done((bf16[4,4,2,8,640]{4,3,2,1,0:T(8,128)(2,1)S(1)}, bf16[4,4,2,8,640]{4,3,2,1,0:T(8,128)(2,1)S(1)}, u32[]{:S(2)}, u32[]{:S(2)}) %collective-permute-start.9) | collective-permute-done | bytes 327712 | tf_op jit(solution)/shard_map/ppermute | solution.py:114
  234.5 19.9 %collective-permute-done.10 = bf16[4,4,2,8,640]{4,3,2,1,0:T(8,128)(2,1)S(1)} collective-permute-done((bf16[4,4,2,8,640]{4,3,2,1,0:T(8,128)(2,1)S(1)}, bf16[4,4,2,8,640]{4,3,2,1,0:T(8,128)(2,1)S(1)}, u32[]{:S(2)}, u32[]{:S(2)}) %collective-permute-start.10) | collective-permute-done | bytes 327712 | tf_op jit(solution)/shard_map/ppermute | solution.py:114
  254.6 6.4 %shard_map.77 = (bf16[8,8,4,640]{3,2,1,0:T(4,128)(2,1)}, bf16[8,8,4,640]{3,2,1,0:T(4,128)(2,1)}, bf16[8,8,4,640]{3,2,1,0:T(4,128)(2,1)}, bf16[8,8,4,640]{3,2,1,0:T(4,128)(2,1)}) custom-call(s32[2]{0:T(128)} %pad_add_fusion.places, bf16[4,4,4,2,8,640]{5,4,3,2,1,0:T(8,128)(2,1)S(1)} %pad_maximum_fusion.2.lat_ref, ...), custom_call_target="tpu_custom_call" | custom-call | tf_op jit(solution)/shard_map/pallas_call | solution.py:92
  (37 shorter events, 9.0 us)
Async XLA Ops:
  56.2 8.2 %copy-start = (bf16[8,8,4,640]{3,2,1,0:T(4,128)(2,1)S(1)}, bf16[8,8,4,640]{3,2,1,0:T(4,128)(2,1)}, u32[]{:S(2)}) copy-start(bf16[8,8,4,640]{3,2,1,0:T(4,128)(2,1)} %param.4) | copy-start | bytes 983044
  56.2 8.2 %copy-start.1 = (bf16[8,8,4,640]{3,2,1,0:T(4,128)(2,1)S(1)}, bf16[8,8,4,640]{3,2,1,0:T(4,128)(2,1)}, u32[]{:S(2)}) copy-start(bf16[8,8,4,640]{3,2,1,0:T(4,128)(2,1)} %param.5) | copy-start | bytes 983044
  56.2 198.4 %all-to-all-start.1 = ((bf16[64,4,1,4,640]{4,3,2,1,0:T(4,128)(2,1)}), bf16[64,4,1,4,640]{4,3,2,1,0:T(4,128)(2,1)}, u32[]{:S(2)}, u32[]{:S(2)}) async-start(bf16[64,4,1,4,640]{4,3,2,1,0:T(4,128)(2,1)} %shard_map.76), calls=%async_computation.1 | async-start | bytes 2621440 | tf_op jit(solution)/shard_map/all_to_all | solution.py:126
  64.2 1.0 copy-start.2
  64.3 1.1 copy-start.3
  65.8 19.9 %collective-permute-start = (bf16[4,4,2,8,640]{4,3,2,1,0:T(8,128)(2,1)S(1)}, bf16[4,4,2,8,640]{4,3,2,1,0:T(8,128)(2,1)S(1)}, u32[]{:S(2)}, u32[]{:S(2)}) collective-permute-start(bf16[4,4,2,8,640]{4,3,2,1,0:T(8,128)(2,1)S(1)} %bitcast.61), channel_id=1, source_target_pairs={{0,256},{64,320},{128,384},{192,448},{256,512},{320,576},{384,640}... | collective-permute-start | bytes 983048 | tf_op jit(solution)/shard_map/ppermute | solution.py:114
  67.7 17.9 %collective-permute-start.1 = (bf16[4,4,2,8,640]{4,3,2,1,0:T(8,128)(2,1)S(1)}, bf16[4,4,2,8,640]{4,3,2,1,0:T(8,128)(2,1)S(1)}, u32[]{:S(2)}, u32[]{:S(2)}) collective-permute-start(bf16[4,4,2,8,640]{4,3,2,1,0:T(8,128)(2,1)S(1)} %bitcast.62), channel_id=1, source_target_pairs={{0,512},{64,576},{128,640},{192,704},{256,768},{320,832},{384,896}... | collective-permute-start | bytes 983048 | tf_op jit(solution)/shard_map/ppermute | solution.py:114
  70.2 18.0 %collective-permute-start.2 = (bf16[4,4,2,8,640]{4,3,2,1,0:T(8,128)(2,1)S(1)}, bf16[4,4,2,8,640]{4,3,2,1,0:T(8,128)(2,1)S(1)}, u32[]{:S(2)}, u32[]{:S(2)}) collective-permute-start(bf16[4,4,2,8,640]{4,3,2,1,0:T(8,128)(2,1)S(1)} %bitcast.63), channel_id=1, source_target_pairs={{0,768},{64,832},{128,896},{192,960},{256,0},{320,64},{384,128},{4... | collective-permute-start | bytes 983048 | tf_op jit(solution)/shard_map/ppermute | solution.py:114
  88.5 32.4 %collective-permute-start.5 = (bf16[4,4,2,8,640]{4,3,2,1,0:T(8,128)(2,1)S(1)}, bf16[4,4,2,8,640]{4,3,2,1,0:T(8,128)(2,1)S(1)}, u32[]{:S(2)}, u32[]{:S(2)}) collective-permute-start(bf16[4,4,2,8,640]{4,3,2,1,0:T(8,128)(2,1)S(1)} %get-tuple-element.12), channel_id=1, source_target_pairs={{0,192},{64,0},{128,64},{192,128},{256,448},{320,256},{384,320},{4... | collective-permute-start | bytes 983048 | tf_op jit(solution)/shard_map/ppermute | solution.py:114
  100.4 46.1 %collective-permute-start.4 = (bf16[4,4,2,8,640]{4,3,2,1,0:T(8,128)(2,1)S(1)}, bf16[4,4,2,8,640]{4,3,2,1,0:T(8,128)(2,1)S(1)}, u32[]{:S(2)}, u32[]{:S(2)}) collective-permute-start(bf16[4,4,2,8,640]{4,3,2,1,0:T(8,128)(2,1)S(1)} %get-tuple-element.13), channel_id=1, source_target_pairs={{0,128},{64,192},{128,0},{192,64},{256,384},{320,448},{384,256},{4... | collective-permute-start | bytes 983048 | tf_op jit(solution)/shard_map/ppermute | solution.py:114
  103.5 56.4 %collective-permute-start.3 = (bf16[4,4,2,8,640]{4,3,2,1,0:T(8,128)(2,1)S(1)}, bf16[4,4,2,8,640]{4,3,2,1,0:T(8,128)(2,1)S(1)}, u32[]{:S(2)}, u32[]{:S(2)}) collective-permute-start(bf16[4,4,2,8,640]{4,3,2,1,0:T(8,128)(2,1)S(1)} %get-tuple-element.14), channel_id=1, source_target_pairs={{0,64},{64,128},{128,192},{192,0},{256,320},{320,384},{384,448},{4... | collective-permute-start | bytes 983048 | tf_op jit(solution)/shard_map/ppermute | solution.py:114
  165.5 19.7 %collective-permute-start.6 = (bf16[4,4,2,8,640]{4,3,2,1,0:T(8,128)(2,1)S(1)}, bf16[4,4,2,8,640]{4,3,2,1,0:T(8,128)(2,1)S(1)}, u32[]{:S(2)}, u32[]{:S(2)}) collective-permute-start(bf16[4,4,2,8,640]{4,3,2,1,0:T(8,128)(2,1)S(1)} %get-tuple-element.9), channel_id=1, source_target_pairs={{0,768},{64,832},{128,896},{192,960},{256,0},{320,64},{384,128},{4... | collective-permute-start | bytes 983048 | tf_op jit(solution)/shard_map/ppermute | solution.py:114
  171.1 14.2 %collective-permute-start.7 = (bf16[4,4,2,8,640]{4,3,2,1,0:T(8,128)(2,1)S(1)}, bf16[4,4,2,8,640]{4,3,2,1,0:T(8,128)(2,1)S(1)}, u32[]{:S(2)}, u32[]{:S(2)}) collective-permute-start(bf16[4,4,2,8,640]{4,3,2,1,0:T(8,128)(2,1)S(1)} %get-tuple-element.10), channel_id=1, source_target_pairs={{0,512},{64,576},{128,640},{192,704},{256,768},{320,832},{384,896}... | collective-permute-start | bytes 983048 | tf_op jit(solution)/shard_map/ppermute | solution.py:114
  174.8 16.0 %collective-permute-start.8 = (bf16[4,4,2,8,640]{4,3,2,1,0:T(8,128)(2,1)S(1)}, bf16[4,4,2,8,640]{4,3,2,1,0:T(8,128)(2,1)S(1)}, u32[]{:S(2)}, u32[]{:S(2)}) collective-permute-start(bf16[4,4,2,8,640]{4,3,2,1,0:T(8,128)(2,1)S(1)} %get-tuple-element.11), channel_id=1, source_target_pairs={{0,256},{64,320},{128,384},{192,448},{256,512},{320,576},{384,640}... | collective-permute-start | bytes 983048 | tf_op jit(solution)/shard_map/ppermute | solution.py:114
  190.9 43.6 %collective-permute-start.9 = (bf16[4,4,2,8,640]{4,3,2,1,0:T(8,128)(2,1)S(1)}, bf16[4,4,2,8,640]{4,3,2,1,0:T(8,128)(2,1)S(1)}, u32[]{:S(2)}, u32[]{:S(2)}) collective-permute-start(bf16[4,4,2,8,640]{4,3,2,1,0:T(8,128)(2,1)S(1)} %pad_maximum_fusion.4), channel_id=1, source_target_pairs={{0,192},{64,0},{128,64},{192,128},{256,448},{320,256},{384,320},{4... | collective-permute-start | bytes 983048 | tf_op jit(solution)/shard_map/ppermute | solution.py:114
  202.1 52.3 %collective-permute-start.10 = (bf16[4,4,2,8,640]{4,3,2,1,0:T(8,128)(2,1)S(1)}, bf16[4,4,2,8,640]{4,3,2,1,0:T(8,128)(2,1)S(1)}, u32[]{:S(2)}, u32[]{:S(2)}) collective-permute-start(bf16[4,4,2,8,640]{4,3,2,1,0:T(8,128)(2,1)S(1)} %pad_maximum_fusion.5), channel_id=1, source_target_pairs={{0,128},{64,192},{128,0},{192,64},{256,384},{320,448},{384,256},{4... | collective-permute-start | bytes 983048 | tf_op jit(solution)/shard_map/ppermute | solution.py:114
  205.6 48.9 %collective-permute-start.11 = (bf16[4,4,2,8,640]{4,3,2,1,0:T(8,128)(2,1)S(1)}, bf16[4,4,2,8,640]{4,3,2,1,0:T(8,128)(2,1)S(1)}, u32[]{:S(2)}, u32[]{:S(2)}) collective-permute-start(bf16[4,4,2,8,640]{4,3,2,1,0:T(8,128)(2,1)S(1)} %pad_maximum_fusion.6), channel_id=1, source_target_pairs={{0,64},{64,128},{128,192},{192,0},{256,320},{320,384},{384,448},{4... | collective-permute-start | bytes 983048 | tf_op jit(solution)/shard_map/ppermute | solution.py:114
